TPU v7x, 32 devices: a whole 2x2x4 slice. The times are simulated.
32 devices in a mesh: blk: 4 (over z), sub: 8 (over y, x, core).
Axes of the slice: x: 2, y: 2, z: 4, core: 2. Of those that a mesh axis runs over, the one named last changes fastest.
Arguments:
- fields: float32 [32, 55, 2197], P(('blk', 'sub')), may hold values from -6 to 6
- flux_matrix: float32 [3, 55, 55], replicated, may hold values from -0.875 to 0.875
- inv_jacobian: float32 [32, 3], P(('blk', 'sub')), may hold values from 1 to 4
- neighbour: int32 [32, 6], P(('blk', 'sub')), may hold values from 0 to 31, as said below
- orientation: int32 [32, 6], P(('blk', 'sub')), may hold values from 0 to 7, as said below
- face_order: int32 [32, 6], P(('blk', 'sub')), may hold values from 9 to 13, as said below
Outputs:
- increment: float32 [32, 55, 2197], P(('blk', 'sub'))
Inputs may be any that keep to these rules, and one draw needn't show every extreme that they name: Element g belongs to the device with blk index (g) // 8 and sub index (g) % 8. The neighbour across face 0 (face 1) lies on the device one step lower (higher) along blk, cyclically, with the same sub index; across face 2 (face 3) on the device one step lower (higher) along sub, cyclically, with the same blk index; across faces 4 and 5 on the same device. If h = neighbour[g, f] then neighbour[h, f xor 1] = g, and the faces of one direction pair the elements of two devices one to one. `orientation`: the two sides of a face carry mutually inverse codes under orient. `face_order`: the two sides of a face carry the same order.
All inputs are finite; a program needn't handle non-finite values.
Results may differ from a plain program's by a relative error of at most 0.002.
Values may be sent and summed in bfloat16 or wider, within the bound.
A program may use at most 64 MiB of HBM per device.

v0:
```python
import functools

import jax
import jax.numpy as jnp
import numpy as np
from jax import lax
from jax.experimental import pallas as pl
from jax.experimental.pallas import tpu as pltpu
from jax.sharding import PartitionSpec as P

MESH = pl.DeviceIdType.MESH
BF = jnp.bfloat16
F32 = jnp.float32
ROWS = 64
LANES = 256
TIME_STEP = 0.01


def cheb_np(n):
    idx = np.arange(n)
    x = -np.cos(np.pi * idx / (n - 1))
    c = np.where((idx == 0) | (idx == n - 1), 2.0, 1.0) * np.where(idx % 2 == 0, 1.0, -1.0)
    eye = np.eye(n)
    off = c[:, None] / c[None, :] / (x[:, None] - x[None, :] + eye) * (1.0 - eye)
    return off - np.diag(off.sum(axis=1))


def dct_np(n):
    k = np.arange(n)[:, None]
    j = np.arange(n)[None, :]
    basis = np.cos(np.pi * k * (j + 0.5) / n) * np.sqrt(2.0 / n)
    return basis * np.where(k == 0, np.sqrt(0.5), 1.0)


def hi_lo(matrix):
    full = matrix.astype(np.float32)
    hi = full.astype(BF)
    lo = (full - hi.astype(np.float32)).astype(BF)
    return np.stack([hi, lo])


def wide(matrix):
    return np.pad(matrix, ((0, 0), (0, LANES - matrix.shape[1])))


def tables(n):
    plane = n * n
    d = cheb_np(n)
    c = dct_np(n)
    eye = np.eye(n)
    along_y = np.kron(d.T, eye)
    along_z = np.kron(eye, d.T)
    deriv = hi_lo(np.concatenate([wide(along_y), wide(along_z)], axis=1))
    forward = np.kron(c.T, c.T)
    swapped = forward.reshape(plane, n, n).transpose(0, 2, 1).reshape(plane, plane)
    fwd = hi_lo(np.concatenate([wide(forward), wide(swapped)], axis=1))
    back = hi_lo(wide(np.kron(c, c)))
    lane = np.arange(LANES)
    first = np.where(lane < plane, lane // n, 999)
    second = np.where(lane < plane, lane % n, 999)
    ends = lambda v: np.where(v == 0, -1.0, np.where(v == n - 1, 1.0, 0.0))
    sign = lambda v: np.where(v % 2 == 0, 1.0, -1.0)
    lanes = np.stack(
        [first, second, ends(first), ends(second), sign(first), sign(second), first * 0, first * 0]
    ).astype(np.float32)
    return deriv, fwd, back, lanes, d


def body(
    n, diff, sizes,
    code_ref, order_ref, jac_ref, fields_ref, flux_ref, deriv_ref, fwd_ref, back_ref, lane_ref,
    out_ref,
    xf, xs, xl, zs, zl, zyz, zx, own, remote, fc, send_sem, recv_sem,
):
    width = fields_ref.shape[1]
    plane = n * n
    last = n - 1
    blk, sub = lax.axis_index("blk"), lax.axis_index("sub")
    n_blk, n_sub = sizes
    across = [
        (lax.rem(blk + n_blk - 1, n_blk), sub),
        (lax.rem(blk + 1, n_blk), sub),
        (blk, lax.rem(sub + n_sub - 1, n_sub)),
        (blk, lax.rem(sub + 1, n_sub)),
    ]
    barrier = pltpu.get_barrier_semaphore()
    for device in across:
        pl.semaphore_signal(barrier, inc=1, device_id=device, device_id_type=MESH)

    first = lane_ref[0:1, :]
    second = lane_ref[1:2, :]

    for i in range(n):
        slab = fields_ref[0, :, plane * i : plane * (i + 1)]
        slab = jnp.pad(slab, ((0, ROWS - width), (0, LANES - plane)))
        xf[i] = slab
        xs[i] = slab.astype(BF)
        xl[i] = (slab - slab.astype(BF).astype(F32)).astype(BF)
    stack = xs[...].reshape(n * ROWS, LANES)[:, :plane]
    stack_lo = xl[...].reshape(n * ROWS, LANES)[:, :plane]

    own[0] = xs[0]
    own[1] = xs[last]
    row_id = lax.broadcasted_iota(jnp.int32, (plane, LANES), 0).astype(F32)
    starts = [second, second + n * last, second * n, second * n + last]

    def trace(face):
        pick = jnp.where(row_id == starts[face - 2], 1.0, 0.0).astype(BF)
        spread = jnp.dot(stack, pick, preferred_element_type=F32).reshape(n, ROWS, LANES)
        total = jnp.zeros((ROWS, LANES), F32)
        for i in range(n):
            total = jnp.where(first == float(i), spread[i], total)
        own[face] = total.astype(BF)

    trace(2)
    trace(3)
    pl.semaphore_wait(barrier, 4)
    copies = []
    for face in range(4):
        copy = pltpu.make_async_remote_copy(
            src_ref=own.at[face],
            dst_ref=remote.at[face ^ 1],
            send_sem=send_sem.at[face],
            recv_sem=recv_sem.at[face ^ 1],
            device_id=across[face],
            device_id_type=MESH,
        )
        copy.start()
        copies.append(copy)
    trace(4)
    trace(5)

    fc[...] = jnp.zeros_like(fc)
    for axis in range(3):
        scaled = flux_ref[axis] * (-TIME_STEP * jac_ref[0, axis])
        fc[axis, 0:width, 0:width] = scaled
    flux = jnp.concatenate([fc[0], fc[1], fc[2]], axis=1)
    flux_hi = flux.astype(BF)
    flux_lo = (flux - flux_hi.astype(F32)).astype(BF)
    flux_both = jnp.concatenate([flux_hi, flux_lo], axis=0)

    zyz[...] = (
        jnp.dot(stack, deriv_ref[0], preferred_element_type=F32)
        + jnp.dot(stack, deriv_ref[1], preferred_element_type=F32)
        + jnp.dot(stack_lo, deriv_ref[0], preferred_element_type=F32)
    ).reshape(n, ROWS, 2 * LANES)

    for r in range(0, ROWS, 16):
        for c in range(0, LANES, 128):
            parts = [xf[a, r : r + 16, c : c + 128] for a in range(n)]
            for i in range(n):
                total = parts[0] * float(diff[i, 0])
                for a in range(1, n):
                    total = total + parts[a] * float(diff[i, a])
                zx[i, r : r + 16, c : c + 128] = total

    own_flat = own[...].reshape(6 * ROWS, LANES)[:, :plane]
    own_modes = (
        jnp.dot(own_flat, fwd_ref[0, :, :LANES], preferred_element_type=F32)
        + jnp.dot(own_flat, fwd_ref[1, :, :LANES], preferred_element_type=F32)
    ).reshape(6, ROWS, LANES)

    for copy in copies:
        copy.wait()

    far = jnp.concatenate([remote[...], own[5:6], own[4:5]], axis=0)
    far = far.reshape(6 * ROWS, LANES)[:, :plane]
    far_modes = (
        jnp.dot(far, fwd_ref[0], preferred_element_type=F32)
        + jnp.dot(far, fwd_ref[1], preferred_element_type=F32)
    ).reshape(6, ROWS, 2 * LANES)
    ones = jnp.ones((1, LANES), F32)
    sign_first = lane_ref[4:5, :]
    sign_second = lane_ref[5:6, :]
    modes = []
    for face in range(6):
        code = code_ref[0, face]
        order = order_ref[0, face].astype(F32)
        swap = code >= 4
        rev_a = lax.rem(lax.div(code, 2), 2)
        rev_b = lax.rem(code, 2)
        use_first = jnp.where(swap, rev_b, rev_a) == 1
        use_second = jnp.where(swap, rev_a, rev_b) == 1
        sign = jnp.where(use_first, sign_first, ones) * jnp.where(use_second, sign_second, ones)
        keep = jnp.where((first < order) & (second < order), 1.0, 0.0)
        turned = jnp.where(swap, far_modes[face, :, LANES:], far_modes[face, :, :LANES])
        modes.append((turned * sign - own_modes[face]) * keep)
    modes = jnp.concatenate(modes, axis=0)[:, :plane]
    modes_hi = modes.astype(BF)
    modes_lo = (modes - modes_hi.astype(F32)).astype(BF)
    modes = modes_hi
    jump = (
        jnp.dot(modes_lo, back_ref[0], preferred_element_type=F32)
        + jnp.dot(modes, back_ref[0], preferred_element_type=F32)
        + jnp.dot(modes, back_ref[1], preferred_element_type=F32)
    ).reshape(6, ROWS, LANES)
    lift = 0.5 * last * last * 0.5
    jump = jump * lift

    row_int = lax.broadcasted_iota(jnp.int32, (plane, LANES), 0)
    row_second = row_int - n * lax.div(row_int, n)
    col = lax.broadcasted_iota(jnp.int32, (plane, LANES), 1)
    places = [row_second, row_second + n * last, row_second * n, row_second * n + last]
    blocks = [[], [], [], []]
    for f in range(4):
        for i in range(n):
            blocks[f].append(jnp.where(first == float(i), jump[f + 2], 0.0).astype(BF))
    scat = []
    for axis in range(2):
        total = None
        for side in range(2):
            f = 2 * axis + side
            put = jnp.where(col == places[f], 1.0 if side else -1.0, 0.0).astype(BF)
            part = jnp.dot(
                jnp.concatenate(blocks[f], axis=0)[:, :plane], put, preferred_element_type=F32
            )
            total = part if total is None else total + part
        scat.append(total.reshape(n, ROWS, LANES))

    gain_y = lane_ref[2:3, :] * (TIME_STEP * jac_ref[0, 1])
    gain_z = lane_ref[3:4, :] * (TIME_STEP * jac_ref[0, 2])
    gain_x = TIME_STEP * jac_ref[0, 0]
    zx[0] = zx[0] - jump[0]
    zx[last] = zx[last] + jump[1]

    def keep_both(i, axis, value):
        hi = value.astype(BF)
        zs[i, axis] = hi
        zl[i, axis] = (value - hi.astype(F32)).astype(BF)

    for i in range(n):
        keep_both(i, 0, zx[i])
        keep_both(i, 1, zyz[i, :, :LANES] + scat[0][i])
        keep_both(i, 2, zyz[i, :, LANES:] + scat[1][i])
        both = jnp.dot(
            flux_both, zs[i].reshape(3 * ROWS, LANES), preferred_element_type=F32
        )
        moved = both[:ROWS] + both[ROWS:] + jnp.dot(
            flux_hi, zl[i].reshape(3 * ROWS, LANES), preferred_element_type=F32
        )
        moved = moved + scat[0][i] * gain_y + scat[1][i] * gain_z
        if i == 0:
            moved = moved + jump[0] * gain_x
        if i == last:
            moved = moved + jump[1] * gain_x
        out_ref[0, :, plane * i : plane * (i + 1)] = moved[:width, :plane]


def solution(mesh):
    sizes = (mesh.shape["blk"], mesh.shape["sub"])

    def on_device(fields, flux_matrix, inv_jacobian, neighbour, orientation, face_order):
        points = fields.shape[2]
        n = round(points ** (1.0 / 3.0))
        deriv, fwd, back, lanes, diff = tables(n)
        smem = pl.BlockSpec(memory_space=pltpu.SMEM)
        vmem = pl.BlockSpec(memory_space=pltpu.VMEM)
        return pl.pallas_call(
            functools.partial(body, n, diff, sizes),
            out_shape=jax.ShapeDtypeStruct(fields.shape, F32),
            in_specs=[smem] * 3 + [vmem] * 6,
            out_specs=vmem,
            scratch_shapes=[
                pltpu.VMEM((n, ROWS, LANES), F32),
                pltpu.VMEM((n, ROWS, LANES), BF),
                pltpu.VMEM((n, ROWS, LANES), BF),
                pltpu.VMEM((n, 3, ROWS, LANES), BF),
                pltpu.VMEM((n, 3, ROWS, LANES), BF),
                pltpu.VMEM((n, ROWS, 2 * LANES), F32),
                pltpu.VMEM((n, ROWS, LANES), F32),
                pltpu.VMEM((6, ROWS, LANES), BF),
                pltpu.VMEM((4, ROWS, LANES), BF),
                pltpu.VMEM((3, ROWS, ROWS), F32),
                pltpu.SemaphoreType.DMA((4,)),
                pltpu.SemaphoreType.DMA((4,)),
            ],
            compiler_params=pltpu.CompilerParams(
                collective_id=0, has_side_effects=True, vmem_limit_bytes=48 * 1024 * 1024
            ),
        )(
            orientation, face_order, inv_jacobian, fields, flux_matrix,
            jnp.asarray(deriv), jnp.asarray(fwd), jnp.asarray(back), jnp.asarray(lanes),
        )

    return jax.shard_map(
        on_device,
        mesh=mesh,
        in_specs=(
            P(("blk", "sub"), None, None),
            P(),
            P(("blk", "sub"), None),
            P(("blk", "sub"), None),
            P(("blk", "sub"), None),
            P(("blk", "sub"), None),
        ),
        out_specs=P(("blk", "sub"), None, None),
        check_vma=False,
    )
```

profile of v0, /device:TPU:0, one launch (start us, length us, event | category | flops | bytes accessed | tf_op | source)
XLA Modules:
  0.0 14.6 jit_solution(6421377789008869360)
XLA Ops:
  0.0 0.0 copy-start
  0.0 0.0 copy-start.1
  0.0 0.0 copy-start.2
  0.0 0.0 copy-start.4
  0.0 0.0 copy-start.6
  0.0 0.0 copy-start.5
  0.0 0.0 copy-start.7
  0.0 0.0 copy-start.3
  0.0 1.2 %copy.10.fields_ref = f32[1,55,2197]{2,1,0:T(8,128)S(1)} copy(f32[1,55,2197]{2,0,1:T(1,128)} %param.10) | data formatting | bytes 966680 | tf_op args[0]
  1.2 0.0 copy-done
  1.2 0.0 copy-done.1
  1.2 0.0 copy-done.2
  1.3 0.0 copy-done.4
  1.3 0.0 copy-done.6
  1.3 0.0 copy-done.5
  1.3 0.0 copy-done.7
  1.3 0.1 copy-done.3
  1.4 11.9 %shard_map.91 = f32[1,55,2197]{2,1,0:T(8,128)S(1)} custom-call(s32[1,6]{1,0:T(1,128)S(1)} %copy-done.5, s32[1,6]{1,0:T(1,128)S(1)} %copy-done.6, f32[1,3]{1,0:T(1,128)S(1)} %copy-done.7, f32[1,55,2197]{2,1,0:T(8,128)S(1)} %copy.10.fields_ref, f32[3,55,55]{2,1,0:T(8,128)S(1)} %copy-done.3, bf16[2,169,512]{2,1,0:T(8,128)(2,1)S(1)} %copy-done.1, ...), custom_call_target="tpu_custom_call" | custom-call | tf_op jit(solution)/shard_map/pallas_call | solution.py:258
  13.3 1.3 %copy.11 = f32[1,55,2197]{2,0,1:T(1,128)} copy(f32[1,55,2197]{2,1,0:T(8,128)S(1)} %shard_map.91) | data formatting | bytes 966680 | tf_op jit(solution)/shard_map/pallas_call | solution.py:258
Async XLA Ops:
  0.0 1.2 %copy-start = (bf16[2,169,512]{2,1,0:T(8,128)(2,1)S(1)}, bf16[2,169,512]{2,1,0:T(8,128)(2,1)}, u32[]{:S(2)}) copy-start(bf16[2,169,512]{2,1,0:T(8,128)(2,1)} %constant.9.clone.fwd_ref) | copy-start | bytes 1038340
  0.0 1.2 %copy-start.1 = (bf16[2,169,512]{2,1,0:T(8,128)(2,1)S(1)}, bf16[2,169,512]{2,1,0:T(8,128)(2,1)}, u32[]{:S(2)}) copy-start(bf16[2,169,512]{2,1,0:T(8,128)(2,1)} %constant.8.clone.deriv_ref) | copy-start | bytes 1038340
  0.0 1.3 %copy-start.2 = (bf16[2,169,256]{2,1,0:T(8,128)(2,1)S(1)}, bf16[2,169,256]{2,1,0:T(8,128)(2,1)}, u32[]{:S(2)}) copy-start(bf16[2,169,256]{2,1,0:T(8,128)(2,1)} %constant.10.clone.back_ref) | copy-start | bytes 519172
  0.0 1.3 %copy-start.4 = (f32[8,256]{1,0:T(8,128)S(1)}, f32[8,256]{1,0:T(8,128)}, u32[]{:S(2)}) copy-start(f32[8,256]{1,0:T(8,128)} %constant.11.clone.lane_ref) | copy-start | bytes 24580
  0.0 1.3 %copy-start.6 = (s32[1,6]{1,0:T(1,128)S(1)}, s32[1,6]{1,0:T(1,128)}, u32[]{:S(2)}) copy-start(s32[1,6]{1,0:T(1,128)} %order_ref.1) | copy-start | bytes 76
  0.0 1.3 %copy-start.5 = (s32[1,6]{1,0:T(1,128)S(1)}, s32[1,6]{1,0:T(1,128)}, u32[]{:S(2)}) copy-start(s32[1,6]{1,0:T(1,128)} %code_ref.1) | copy-start | bytes 76
  0.0 1.3 %copy-start.7 = (f32[1,3]{1,0:T(1,128)S(1)}, f32[1,3]{1,0:T(1,128)}, u32[]{:S(2)}) copy-start(f32[1,3]{1,0:T(1,128)} %jac_ref.1) | copy-start | bytes 40
  0.0 1.3 %copy-start.3 = (f32[3,55,55]{2,1,0:T(8,128)S(1)}, f32[3,55,55]{2,1,0:T(8,128)}, u32[]{:S(2)}) copy-start(f32[3,55,55]{2,1,0:T(8,128)} %flux_ref.1) | copy-start | bytes 108904
where the time goes:
time: 14.7 us; the launch traced here: 14.6 us
  Pallas kernels  11.9 us (81%)
  local copies, waits for them, and re-layouts  2.64 us (18%)
    pallas_call x1, Pallas kernels, on_device(): pl.pallas_call(functools.partial(body, n, diff, sizes), out_shape=jax.Sha...  11.9 us
    unnamed x17, local copies, waits for them, and re-layouts  1.33 us
    pallas_call x1, local copies, waits for them, and re-layouts, on_device(): pl.pallas_call(functools.partial(body, n, diff, sizes), out_shape=jax.Sha...  1.31 us

commit v1 on v0

--- a/solution.py
+++ b/solution.py
@@ -13,6 +13,7 @@
 F32 = jnp.float32
 ROWS = 64
 LANES = 256
+ENTRY = (1, 3)
 TIME_STEP = 0.01
 
 
@@ -68,11 +69,12 @@
 
 def body(
     n, diff, sizes,
+    code_hbm, order_hbm, jac_hbm, fields_hbm, flux_hbm, deriv_hbm, fwd_hbm, back_hbm, lane_hbm,
+    out_ref,
     code_ref, order_ref, jac_ref, fields_ref, flux_ref, deriv_ref, fwd_ref, back_ref, lane_ref,
-    out_ref,
-    xf, xs, xl, zs, zl, zyz, zx, own, remote, fc, send_sem, recv_sem,
+    xf, xs, xl, zs, zl, zyz, zx, own, remote, fc, load_sem, send_sem, recv_sem, ack,
 ):
-    width = fields_ref.shape[1]
+    width = fields_ref.shape[0]
     plane = n * n
     last = n - 1
     blk, sub = lax.axis_index("blk"), lax.axis_index("sub")
@@ -84,14 +86,24 @@
         (blk, lax.rem(sub + 1, n_sub)),
     ]
     barrier = pltpu.get_barrier_semaphore()
-    for device in across:
-        pl.semaphore_signal(barrier, inc=1, device_id=device, device_id_type=MESH)
+    for face in ENTRY:
+        pl.semaphore_signal(barrier, inc=1, device_id=across[face ^ 1], device_id_type=MESH)
+    pairs = [
+        (fields_hbm.at[:, 0, :], fields_ref), (lane_hbm, lane_ref), (deriv_hbm, deriv_ref),
+        (fwd_hbm, fwd_ref), (flux_hbm, flux_ref), (back_hbm, back_ref),
+        (jac_hbm, jac_ref), (code_hbm, code_ref), (order_hbm, order_ref),
+    ]
+    loads = [pltpu.make_async_copy(a, b, load_sem.at[i]) for i, (a, b) in enumerate(pairs)]
+    for load in loads:
+        load.start()
+    loads[0].wait()
+    loads[1].wait()
 
     first = lane_ref[0:1, :]
     second = lane_ref[1:2, :]
 
     for i in range(n):
-        slab = fields_ref[0, :, plane * i : plane * (i + 1)]
+        slab = fields_ref[:, plane * i : plane * (i + 1)]
         slab = jnp.pad(slab, ((0, ROWS - width), (0, LANES - plane)))
         xf[i] = slab
         xs[i] = slab.astype(BF)
@@ -112,12 +124,8 @@
             total = jnp.where(first == float(i), spread[i], total)
         own[face] = total.astype(BF)
 
-    trace(2)
-    trace(3)
-    pl.semaphore_wait(barrier, 4)
-    copies = []
-    for face in range(4):
-        copy = pltpu.make_async_remote_copy(
+    copies = [
+        pltpu.make_async_remote_copy(
             src_ref=own.at[face],
             dst_ref=remote.at[face ^ 1],
             send_sem=send_sem.at[face],
@@ -125,10 +133,34 @@
             device_id=across[face],
             device_id_type=MESH,
         )
-        copy.start()
-        copies.append(copy)
+        for face in range(4)
+    ]
+    pl.semaphore_wait(barrier, 2)
+    copies[1].start()
+    for face in ENTRY:
+        pl.semaphore_signal(ack.at[face ^ 1], inc=1, device_id=across[face], device_id_type=MESH)
+    trace(2)
+    trace(3)
+    copies[3].start()
+
+    def answer(face):
+        pl.semaphore_wait(ack.at[face], 1)
+        copies[face].start()
+
+    @pl.when(lax.rem(sub, 2) == 0)
+    def _():
+        answer(0)
+        answer(2)
+
+    @pl.when(lax.rem(sub, 2) == 1)
+    def _():
+        answer(2)
+        answer(0)
+
     trace(4)
     trace(5)
+    for load in loads[2:]:
+        load.wait()
 
     fc[...] = jnp.zeros_like(fc)
     for axis in range(3):
@@ -243,24 +275,39 @@
             moved = moved + jump[0] * gain_x
         if i == last:
             moved = moved + jump[1] * gain_x
-        out_ref[0, :, plane * i : plane * (i + 1)] = moved[:width, :plane]
+        out_ref[:, plane * i : plane * (i + 1)] = moved[:width, :plane]
+
+
+def hand_over(part_ref, out_ref, sem):
+    copy = pltpu.make_async_copy(part_ref, out_ref.at[:, 0, :], sem)
+    copy.start()
+    copy.wait()
 
 
 def solution(mesh):
     sizes = (mesh.shape["blk"], mesh.shape["sub"])
 
     def on_device(fields, flux_matrix, inv_jacobian, neighbour, orientation, face_order):
-        points = fields.shape[2]
+        width, points = fields.shape[1:]
         n = round(points ** (1.0 / 3.0))
         deriv, fwd, back, lanes, diff = tables(n)
-        smem = pl.BlockSpec(memory_space=pltpu.SMEM)
-        vmem = pl.BlockSpec(memory_space=pltpu.VMEM)
-        return pl.pallas_call(
+        rows = jnp.transpose(fields, (1, 0, 2))
+        hbm = pl.BlockSpec(memory_space=pltpu.HBM)
+        operands = [
+            orientation, face_order, inv_jacobian, rows, flux_matrix,
+            jnp.asarray(deriv), jnp.asarray(fwd), jnp.asarray(back), jnp.asarray(lanes),
+        ]
+        smem = lambda a: pltpu.SMEM(a.shape, a.dtype)
+        vmem = lambda a: pltpu.VMEM(a.shape, a.dtype)
+        part = pl.pallas_call(
             functools.partial(body, n, diff, sizes),
-            out_shape=jax.ShapeDtypeStruct(fields.shape, F32),
-            in_specs=[smem] * 3 + [vmem] * 6,
-            out_specs=vmem,
-            scratch_shapes=[
+            out_shape=pltpu.VMEM((width, points), F32),
+            in_specs=[hbm] * 9,
+            out_specs=pl.BlockSpec(memory_space=pltpu.VMEM),
+            scratch_shapes=[smem(a) for a in operands[:3]]
+            + [pltpu.VMEM((width, points), F32)]
+            + [vmem(a) for a in operands[4:]]
+            + [
                 pltpu.VMEM((n, ROWS, LANES), F32),
                 pltpu.VMEM((n, ROWS, LANES), BF),
                 pltpu.VMEM((n, ROWS, LANES), BF),
@@ -271,16 +318,24 @@
                 pltpu.VMEM((6, ROWS, LANES), BF),
                 pltpu.VMEM((4, ROWS, LANES), BF),
                 pltpu.VMEM((3, ROWS, ROWS), F32),
+                pltpu.SemaphoreType.DMA((9,)),
                 pltpu.SemaphoreType.DMA((4,)),
                 pltpu.SemaphoreType.DMA((4,)),
+                pltpu.SemaphoreType.REGULAR((4,)),
             ],
             compiler_params=pltpu.CompilerParams(
                 collective_id=0, has_side_effects=True, vmem_limit_bytes=48 * 1024 * 1024
             ),
-        )(
-            orientation, face_order, inv_jacobian, fields, flux_matrix,
-            jnp.asarray(deriv), jnp.asarray(fwd), jnp.asarray(back), jnp.asarray(lanes),
-        )
+        )(*[pltpu.with_memory_space_constraint(a, pltpu.HBM) for a in operands])
+        out = pl.pallas_call(
+            hand_over,
+            out_shape=jax.ShapeDtypeStruct(rows.shape, F32),
+            in_specs=[pl.BlockSpec(memory_space=pltpu.VMEM)],
+            out_specs=hbm,
+            scratch_shapes=[pltpu.SemaphoreType.DMA],
+            compiler_params=pltpu.CompilerParams(vmem_limit_bytes=16 * 1024 * 1024),
+        )(part)
+        return jnp.transpose(out, (1, 0, 2))
 
     return jax.shard_map(
         on_device,

time: 14.7 us -> 12.2 us (0.83)
  the two profiles are of different devices: /device:TPU:0 before, /device:TPU:1 now
where the time goes in v1:
time: 12.2 us; the launch traced here: 12.1 us
  Pallas kernels  12.1 us (99%)
    pallas_call x1, Pallas kernels, on_device(): pl.pallas_call(functools.partial(body, n, diff, sizes), out_shape=pltpu.V...  11.3 us
    pallas_call x1, Pallas kernels, on_device(): pl.pallas_call(hand_over, out_shape=jax.ShapeDtypeStruct(rows.shape, F32)...  0.78 us

profile of v1, /device:TPU:1, one launch (start us, length us, event | category | flops | bytes accessed | tf_op | source)
XLA Modules:
  0.0 12.1 jit_solution(8843681581906746295)
XLA Ops:
  0.0 11.3 %shard_map.91.part_ref = f32[55,2197]{1,0:T(8,128)S(1)} custom-call(s32[1,6]{1,0:T(1,128)} %code_hbm.1, s32[1,6]{1,0:T(1,128)} %order_hbm.1, f32[1,3]{1,0:T(1,128)} %jac_hbm.1, f32[55,1,2197]{2,1,0:T(1,128)} %bitcast.2, f32[3,55,55]{2,1,0:T(8,128)} %flux_hbm.1, bf16[2,169,512]{2,1,0:T(8,128)(2,1)} %constant.8.clone.deriv_hbm, ...), custom_call_target="tpu_custom_call" | custom-call | tf_op jit(solution)/shard_map/pallas_call | solution.py:302
  11.3 0.8 %shard_map.92 = f32[55,1,2197]{2,1,0:T(1,128)} custom-call(f32[55,2197]{1,0:T(8,128)S(1)} %shard_map.91.part_ref), custom_call_target="tpu_custom_call" | custom-call | tf_op jit(solution)/shard_map/pallas_call | solution.py:330

commit v2 on v1

v2 whole, which is shorter than its diff:
```python
import functools

import jax
import jax.numpy as jnp
import numpy as np
from jax import lax
from jax.experimental import pallas as pl
from jax.experimental.pallas import tpu as pltpu
from jax.sharding import PartitionSpec as P

MESH = pl.DeviceIdType.MESH
BF = jnp.bfloat16
F32 = jnp.float32
ROWS = 64
LANES = 256
TIME_STEP = 0.01
ENTRY = (1, 3)


def cheb_np(n):
    idx = np.arange(n)
    x = -np.cos(np.pi * idx / (n - 1))
    c = np.where((idx == 0) | (idx == n - 1), 2.0, 1.0) * np.where(idx % 2 == 0, 1.0, -1.0)
    eye = np.eye(n)
    off = c[:, None] / c[None, :] / (x[:, None] - x[None, :] + eye) * (1.0 - eye)
    return off - np.diag(off.sum(axis=1))


def dct_np(n):
    k = np.arange(n)[:, None]
    j = np.arange(n)[None, :]
    basis = np.cos(np.pi * k * (j + 0.5) / n) * np.sqrt(2.0 / n)
    return basis * np.where(k == 0, np.sqrt(0.5), 1.0)


def hi_lo(matrix):
    full = matrix.astype(np.float32)
    hi = full.astype(BF)
    lo = (full - hi.astype(np.float32)).astype(BF)
    return np.stack([hi, lo])


def wide(matrix, lanes=LANES):
    return np.pad(matrix, ((0, 0), (0, lanes - matrix.shape[1])))


def tables(n):
    plane = n * n
    d = cheb_np(n)
    c = dct_np(n)
    eye = np.eye(n)
    deriv = np.stack([hi_lo(wide(np.kron(d.T, eye))), hi_lo(wide(np.kron(eye, d.T)))])
    forward = np.kron(c.T, c.T)
    swapped = forward.reshape(plane, n, n).transpose(0, 2, 1).reshape(plane, plane)
    fwd = np.stack([hi_lo(wide(forward)), hi_lo(wide(swapped))])
    back = hi_lo(wide(np.kron(c, c)))
    lane = np.arange(LANES)
    first = np.where(lane < plane, lane // n, 999)
    second = np.where(lane < plane, lane % n, 999)
    sign = lambda v: np.where(v % 2 == 0, 1.0, -1.0)
    lanes = np.stack(
        [first, second, sign(first), sign(second)] + [first * 0] * 4
    ).astype(np.float32)
    pick = np.zeros((plane, 2 * n))
    for j in range(n):
        pick[n * j, j] = 1.0
        pick[n * j + n - 1, n + j] = 1.0
    put = np.concatenate([pick.T, pick.T])
    return deriv, fwd, back, lanes, wide(pick, 128).astype(BF), wide(put).astype(BF), d


def split(value):
    hi = value.astype(BF)
    return hi, (value - hi.astype(F32)).astype(BF)


def dot(a, b):
    return jnp.dot(a, b, preferred_element_type=F32)


def body(
    n, diff, sizes,
    code_hbm, order_hbm, jac_hbm, fields_hbm, flux_hbm,
    deriv_hbm, fwd_hbm, back_hbm, lane_hbm, pick_hbm, put_hbm,
    out_ref,
    code_ref, order_ref, jac_ref, fields_ref, flux_ref,
    deriv_ref, fwd_ref, back_ref, lane_ref, pick_ref, put_ref,
    xs, xl, gx, gs, vol, own, remote, raw, mix, lift_lhs, oper, early,
    load_sem, send_sem, recv_sem, ack,
):
    width, points = fields_ref.shape
    plane = n * n
    last = n - 1
    blk, sub = lax.axis_index("blk"), lax.axis_index("sub")
    n_blk, n_sub = sizes
    across = [
        (lax.rem(blk + n_blk - 1, n_blk), sub),
        (lax.rem(blk + 1, n_blk), sub),
        (blk, lax.rem(sub + n_sub - 1, n_sub)),
        (blk, lax.rem(sub + 1, n_sub)),
    ]
    barrier = pltpu.get_barrier_semaphore()
    for face in ENTRY:
        pl.semaphore_signal(barrier, inc=1, device_id=across[face ^ 1], device_id_type=MESH)
    low = -(-plane // 128) * 128
    high = plane * last // 128 * 128
    piece = lambda a, b: (fields_hbm.at[:, 0, a:b], fields_ref.at[:, a:b])
    pairs = [
        piece(0, low), piece(high, points), piece(low, high),
        (pick_hbm, pick_ref), (fwd_hbm, fwd_ref), (lane_hbm, lane_ref), (back_hbm, back_ref),
        (flux_hbm, flux_ref), (deriv_hbm, deriv_ref), (put_hbm, put_ref),
        (jac_hbm, jac_ref), (code_hbm, code_ref), (order_hbm, order_ref),
    ]
    loads = [pltpu.make_async_copy(a, b, load_sem.at[i]) for i, (a, b) in enumerate(pairs)]
    for load in loads:
        load.start()
    copies = [
        pltpu.make_async_remote_copy(
            src_ref=own.at[face],
            dst_ref=remote.at[face ^ 1],
            send_sem=send_sem.at[face],
            recv_sem=recv_sem.at[face ^ 1],
            device_id=across[face],
            device_id_type=MESH,
        )
        for face in range(4)
    ]

    def padded(value):
        return jnp.pad(value, ((0, ROWS - value.shape[0]), (0, LANES - value.shape[1])))

    def slab(i):
        return padded(fields_ref[:, plane * i : plane * (i + 1)])

    loads[0].wait()
    loads[1].wait()
    own[0] = slab(0).astype(BF)
    own[1] = slab(last).astype(BF)
    pl.semaphore_wait(barrier, 2)
    copies[1].start()
    for face in ENTRY:
        pl.semaphore_signal(ack.at[face ^ 1], inc=1, device_id=across[face], device_id_type=MESH)
    loads[2].wait()
    for face in (2, 3):
        at = (face - 2) * (plane - n)
        runs = [fields_ref[:, plane * i + at : plane * i + at + n] for i in range(n)]
        own[face] = padded(jnp.concatenate(runs, axis=1)).astype(BF)
    copies[3].start()

    for i in range(n):
        xs[i], xl[i] = split(slab(i))
    stack = xs[...].reshape(n * ROWS, LANES)[:, :plane]
    loads[3].wait()
    ends = dot(stack, pick_ref[...]).reshape(n, ROWS, 128)
    for face in (4, 5):
        at = (face - 4) * n
        runs = [ends[i, :, at : at + n] for i in range(n)]
        own[face] = padded(jnp.concatenate(runs, axis=1)).astype(BF)

    def answer(face):
        pl.semaphore_wait(ack.at[face], 1)
        copies[face].start()

    y_first = jnp.logical_or(lax.rem(sub, 2) == 1, blk == 0)

    @pl.when(y_first)
    def _():
        answer(2)

    @pl.when(jnp.logical_not(y_first))
    def _():
        answer(0)

    for load in loads[4:]:
        load.wait()

    raw[...] = jnp.zeros_like(raw)
    for axis in range(3):
        scaled = flux_ref[axis] * (-TIME_STEP * jac_ref[0, axis])
        for k in range(3):
            raw[axis, 0:width, ROWS * k : ROWS * k + width] = scaled

    def thirds(value):
        lane = lax.broadcasted_iota(jnp.int32, value.shape, value.ndim - 1)
        hi = value.astype(BF).astype(F32)
        return jnp.where(lane < 2 * ROWS, hi, value - hi).astype(BF)

    mix[...] = thirds(raw[...])
    row = lax.broadcasted_iota(jnp.int32, (ROWS, LANES), 0)
    lane = lax.broadcasted_iota(jnp.int32, (ROWS, LANES), 1)
    diagonal = jnp.logical_and(jnp.bitwise_and(lane, ROWS - 1) == row, lane < 3 * ROWS)
    lift = 0.5 * last * last * 0.5
    for face in range(6):
        side = lift if face % 2 else -lift
        keep = lift * TIME_STEP * jac_ref[0, face // 2]
        lift_lhs[face] = thirds(raw[face // 2] * side + jnp.where(diagonal, keep, 0.0))

    def fluxed(lhs, hi, lo):
        return dot(lhs[:, : 3 * ROWS], jnp.concatenate([hi, lo, hi], axis=0))

    for i in range(n):
        mixed = fluxed(mix[...].reshape(3 * ROWS, LANES), xs[i], xl[i])
        gx[i] = mixed[:ROWS]
        for axis in range(2):
            part = mixed[ROWS * (axis + 1) : ROWS * (axis + 2)]
            gs[axis, 0, i], gs[axis, 1, i] = split(part)

    first = lane_ref[0:1, :]
    second = lane_ref[1:2, :]
    ones = jnp.ones((1, LANES), F32)

    def face_facts(face):
        code = code_ref[0, face]
        order = order_ref[0, face].astype(F32)
        swap = jnp.where(code >= 4, 1, 0)
        rev_a = lax.rem(lax.div(code, 2), 2)
        rev_b = lax.rem(code, 2)
        use_first = jnp.where(swap == 1, rev_b, rev_a) == 1
        use_second = jnp.where(swap == 1, rev_a, rev_b) == 1
        sign = jnp.where(use_first, lane_ref[2:3, :], ones) * jnp.where(
            use_second, lane_ref[3:4, :], ones
        )
        keep = jnp.where((first < order) & (second < order), 1.0, 0.0)
        return swap, sign, keep

    facts = [face_facts(face) for face in range(6)]
    own_flat = own[...].reshape(6 * ROWS, LANES)[:, :plane]
    own_modes = (dot(own_flat, fwd_ref[0, 0]) + dot(own_flat, fwd_ref[0, 1])).reshape(
        6, ROWS, LANES
    )
    modes = []
    for face in range(6):
        swap, sign, keep = facts[face]
        if face < 4:
            modes.append(own_modes[face] * -keep)
        else:
            far = own[face ^ 1][:, :plane]
            turned = dot(far, fwd_ref[swap, 0]) + dot(far, fwd_ref[swap, 1])
            modes.append((turned * sign - own_modes[face]) * keep)
    modes_hi, modes_lo = split(jnp.concatenate(modes, axis=0))
    modes_hi, modes_lo = modes_hi[:, :plane], modes_lo[:, :plane]
    jump = dot(modes_hi, back_ref[0]) + dot(modes_lo, back_ref[0]) + dot(modes_hi, back_ref[1])
    jump_hi, jump_lo = split(jump)
    cut = lambda a, f: a[ROWS * f : ROWS * (f + 1)]
    lifted = [
        fluxed(lift_lhs[face], cut(jump_hi, face), cut(jump_lo, face)) for face in range(6)
    ]
    for face in range(4):
        early[face] = lifted[face]

    @pl.when(y_first)
    def _():
        answer(0)

    @pl.when(jnp.logical_not(y_first))
    def _():
        answer(2)

    for face in range(4):
        swap, sign, keep = facts[face]
        scale = sign * keep
        f_hi = (fwd_ref[swap, 0].astype(F32) * scale).astype(BF)[:, :plane]
        f_lo = (fwd_ref[swap, 1].astype(F32) * scale).astype(BF)[:, :plane]
        whole = dot(f_hi, back_ref[0]) + dot(f_lo, back_ref[0]) + dot(f_hi, back_ref[1])
        oper[face, 0], oper[face, 1] = split(whole)

    runs = []
    for i in range(n):
        both = jnp.concatenate(
            [lifted[4][:, n * i : n * (i + 1)], lifted[5][:, n * i : n * (i + 1)]], axis=1
        )
        hi = both.astype(BF).astype(F32)
        runs.append(jnp.concatenate([hi, both - hi], axis=1).astype(BF))
    total = dot(jnp.concatenate(runs, axis=0), put_ref[...])
    for axis in range(2):
        hi = gs[axis, 0].reshape(n * ROWS, LANES)[:, :plane]
        lo = gs[axis, 1].reshape(n * ROWS, LANES)[:, :plane]
        total = total + dot(hi, deriv_ref[axis, 0])
        total = total + dot(lo, deriv_ref[axis, 0])
        total = total + dot(hi, deriv_ref[axis, 1])
    vol[...] = total.reshape(n, ROWS, LANES)

    half = n // 2
    for r in range(0, -(-width // 8) * 8, 8):
        for c in range(0, LANES, 128):
            at = (slice(r, r + 8), slice(c, c + 128))
            plus, minus = [], []
            for a in range(half):
                one, two = gx[(a,) + at], gx[(last - a,) + at]
                plus.append(one + two)
                minus.append(one - two)
            middle = gx[(half,) + at]
            for i in range(half):
                even = minus[0] * float(0.5 * (diff[i, 0] - diff[i, last]))
                odd = middle * float(diff[i, half])
                for a in range(half):
                    odd = odd + plus[a] * float(0.5 * (diff[i, a] + diff[i, last - a]))
                    if a:
                        even = even + minus[a] * float(0.5 * (diff[i, a] - diff[i, last - a]))
                vol[(i,) + at] += even + odd
                vol[(last - i,) + at] += even - odd
            even = minus[0] * float(diff[half, 0])
            for a in range(1, half):
                even = even + minus[a] * float(diff[half, a])
            vol[(half,) + at] += even
    for i in range(n):
        value = vol[i]
        if i == 0:
            value = value + early[0]
        if i == last:
            value = value + early[1]
        out_ref[:, plane * i : plane * (i + 1)] = value[:width, :plane]

    def arrived(face):
        copies[face ^ 1].wait_recv()
        far = remote[face][:, :plane]
        turned = dot(far, oper[face, 0]) + dot(far, oper[face, 1])
        return fluxed(lift_lhs[face], *split(turned))

    for face in (2, 3):
        total = (arrived(face) + early[face])[:width]
        at = (face - 2) * (plane - n)
        for i in range(n):
            out_ref[:, plane * i + at : plane * i + at + n] += total[:, n * i : n * (i + 1)]
    for face in (0, 1):
        at = face * plane * last
        out_ref[:, at : at + plane] += arrived(face)[:width, :plane]
    for copy in copies:
        copy.wait_send()


def hand_over(part_ref, out_ref, sem):
    copy = pltpu.make_async_copy(part_ref, out_ref.at[:, 0, :], sem)
    copy.start()
    copy.wait()


def solution(mesh):
    sizes = (mesh.shape["blk"], mesh.shape["sub"])

    def on_device(fields, flux_matrix, inv_jacobian, neighbour, orientation, face_order):
        width, points = fields.shape[1:]
        n = round(points ** (1.0 / 3.0))
        plane = n * n
        *constants, diff = tables(n)
        rows = jnp.transpose(fields, (1, 0, 2))
        hbm = pl.BlockSpec(memory_space=pltpu.HBM)
        operands = [orientation, face_order, inv_jacobian, rows, flux_matrix]
        operands += [jnp.asarray(a) for a in constants]
        vmem = lambda a: pltpu.VMEM(a.shape, a.dtype)
        part = pl.pallas_call(
            functools.partial(body, n, diff, sizes),
            out_shape=pltpu.VMEM((width, points), F32),
            in_specs=[hbm] * len(operands),
            out_specs=pl.BlockSpec(memory_space=pltpu.VMEM),
            scratch_shapes=[pltpu.SMEM(a.shape, a.dtype) for a in operands[:3]]
            + [pltpu.VMEM((width, points), F32)]
            + [vmem(a) for a in operands[4:]]
            + [
                pltpu.VMEM((n, ROWS, LANES), BF),
                pltpu.VMEM((n, ROWS, LANES), BF),
                pltpu.VMEM((n, ROWS, LANES), F32),
                pltpu.VMEM((2, 2, n, ROWS, LANES), BF),
                pltpu.VMEM((n, ROWS, LANES), F32),
                pltpu.VMEM((6, ROWS, LANES), BF),
                pltpu.VMEM((4, ROWS, LANES), BF),
                pltpu.VMEM((3, ROWS, LANES), F32),
                pltpu.VMEM((3, ROWS, LANES), BF),
                pltpu.VMEM((6, ROWS, LANES), BF),
                pltpu.VMEM((4, 2, plane, LANES), BF),
                pltpu.VMEM((4, ROWS, LANES), F32),
                pltpu.SemaphoreType.DMA((13,)),
                pltpu.SemaphoreType.DMA((4,)),
                pltpu.SemaphoreType.DMA((4,)),
                pltpu.SemaphoreType.REGULAR((4,)),
            ],
            compiler_params=pltpu.CompilerParams(
                collective_id=0, has_side_effects=True, vmem_limit_bytes=48 * 1024 * 1024
            ),
        )(*[pltpu.with_memory_space_constraint(a, pltpu.HBM) for a in operands])
        out = pl.pallas_call(
            hand_over,
            out_shape=jax.ShapeDtypeStruct(rows.shape, F32),
            in_specs=[pl.BlockSpec(memory_space=pltpu.VMEM)],
            out_specs=hbm,
            scratch_shapes=[pltpu.SemaphoreType.DMA],
            compiler_params=pltpu.CompilerParams(vmem_limit_bytes=16 * 1024 * 1024),
        )(part)
        return jnp.transpose(out, (1, 0, 2))

    return jax.shard_map(
        on_device,
        mesh=mesh,
        in_specs=(
            P(("blk", "sub"), None, None),
            P(),
            P(("blk", "sub"), None),
            P(("blk", "sub"), None),
            P(("blk", "sub"), None),
            P(("blk", "sub"), None),
        ),
        out_specs=P(("blk", "sub"), None, None),
        check_vma=False,
    )
```

time: 12.2 us -> 10.8 us (0.89)
  the two profiles are of different devices: /device:TPU:1 before, /device:TPU:0 now
where the time goes in v2:
time: 10.8 us; the launch traced here: 10.7 us
  Pallas kernels  10.7 us (99%)
    pallas_call x1, Pallas kernels, on_device(): pl.pallas_call(functools.partial(body, n, diff, sizes), out_shape=pltpu.V...  9.87 us
    pallas_call x1, Pallas kernels, on_device(): pl.pallas_call(hand_over, out_shape=jax.ShapeDtypeStruct(rows.shape, F32)...  0.78 us

profile of v2, /device:TPU:0, one launch (start us, length us, event | category | flops | bytes accessed | tf_op | source)
XLA Modules:
  0.0 10.7 jit_solution(7050306257274390900)
XLA Ops:
  0.0 9.9 %shard_map.109.part_ref = f32[55,2197]{1,0:T(8,128)S(1)} custom-call(s32[1,6]{1,0:T(1,128)} %code_hbm.1, s32[1,6]{1,0:T(1,128)} %order_hbm.1, f32[1,3]{1,0:T(1,128)} %jac_hbm.1, f32[55,1,2197]{2,1,0:T(1,128)} %bitcast.2, f32[3,55,55]{2,1,0:T(8,128)} %flux_hbm.1, bf16[2,2,169,256]{3,2,1,0:T(8,128)(2,1)} %constant.12.clone.deriv_hbm, ...), custom_call_target="tpu_custom_call" | custom-call | tf_op jit(solution)/shard_map/pallas_call | solution.py:351
  9.9 0.8 %shard_map.110 = f32[55,1,2197]{2,1,0:T(1,128)} custom-call(f32[55,2197]{1,0:T(8,128)S(1)} %shard_map.109.part_ref), custom_call_target="tpu_custom_call" | custom-call | tf_op jit(solution)/shard_map/pallas_call | solution.py:381

commit v3 on v2

v3 whole, which is shorter than its diff:
```python
import functools

import jax
import jax.numpy as jnp
import numpy as np
from jax import lax
from jax.experimental import pallas as pl
from jax.experimental.pallas import tpu as pltpu
from jax.sharding import PartitionSpec as P

MESH = pl.DeviceIdType.MESH
BF = jnp.bfloat16
F32 = jnp.float32
ROWS = 64
LANES = 256
TIME_STEP = 0.01
ENTRY = (1, 3)
FIRST = 13


def cheb_np(n):
    idx = np.arange(n)
    x = -np.cos(np.pi * idx / (n - 1))
    c = np.where((idx == 0) | (idx == n - 1), 2.0, 1.0) * np.where(idx % 2 == 0, 1.0, -1.0)
    eye = np.eye(n)
    off = c[:, None] / c[None, :] / (x[:, None] - x[None, :] + eye) * (1.0 - eye)
    return off - np.diag(off.sum(axis=1))


def dct_np(n):
    k = np.arange(n)[:, None]
    j = np.arange(n)[None, :]
    basis = np.cos(np.pi * k * (j + 0.5) / n) * np.sqrt(2.0 / n)
    return basis * np.where(k == 0, np.sqrt(0.5), 1.0)


def hi_lo(matrix):
    full = matrix.astype(np.float32)
    hi = full.astype(BF)
    lo = (full - hi.astype(np.float32)).astype(BF)
    return np.stack([hi, lo])


def wide(matrix, lanes=LANES):
    return np.pad(matrix, ((0, 0), (0, lanes - matrix.shape[1])))


def tables(n):
    plane = n * n
    d = cheb_np(n)
    c = dct_np(n)
    eye = np.eye(n)
    deriv = np.stack([hi_lo(wide(np.kron(d.T, eye))), hi_lo(wide(np.kron(eye, d.T)))])
    forward = np.kron(c.T, c.T)
    swapped = forward.reshape(plane, n, n).transpose(0, 2, 1).reshape(plane, plane)
    fwd = np.stack([hi_lo(wide(forward)), hi_lo(wide(swapped))])
    back = hi_lo(wide(np.kron(c, c)))
    lane = np.arange(LANES)
    first = np.where(lane < plane, lane // n, 999)
    second = np.where(lane < plane, lane % n, 999)
    sign = lambda v: np.where(v % 2 == 0, 1.0, -1.0)
    lanes = np.stack(
        [first, second, sign(first), sign(second)] + [first * 0] * 4
    ).astype(np.float32)
    pick = np.zeros((plane, 2 * n))
    for j in range(n):
        pick[n * j, j] = 1.0
        pick[n * j + n - 1, n + j] = 1.0
    put = np.concatenate([pick.T, pick.T])
    return deriv, fwd, back, lanes, wide(pick, 128).astype(BF), wide(put).astype(BF), d


def split(value):
    hi = value.astype(BF)
    return hi, (value - hi.astype(F32)).astype(BF)


def dot(a, b):
    return jnp.dot(a, b, preferred_element_type=F32)


def fluxed(lhs, hi, lo):
    return dot(lhs[:, : 3 * ROWS], jnp.concatenate([hi, lo, hi], axis=0))


def far_terms(pair, far, oper, lift_lhs):
    plane = oper.shape[2]
    turned = [
        dot(far[f][:, :plane], oper[f, 0]) + dot(far[f][:, :plane], oper[f, 1]) for f in pair
    ]
    return [fluxed(lift_lhs[f], *split(t)) for f, t in zip(pair, turned)]


def body(
    n, diff, sizes,
    code_hbm, order_hbm, jac_hbm, fields_hbm, flux_hbm,
    deriv_hbm, fwd_hbm, back_hbm, lane_hbm, pick_hbm, put_hbm,
    out_ref, far_ref, oper, lift_lhs,
    code_ref, order_ref, jac_ref, fields_ref, flux_ref,
    deriv_ref, fwd_ref, back_ref, lane_ref, pick_ref, put_ref,
    xs, xl, gx, gs, vol, own, remote, raw, mix, early,
    load_sem, send_sem, recv_sem, ack,
):
    width, points = fields_ref.shape
    plane = n * n
    last = n - 1
    blk, sub = lax.axis_index("blk"), lax.axis_index("sub")
    n_blk, n_sub = sizes
    across = [
        (lax.rem(blk + n_blk - 1, n_blk), sub),
        (lax.rem(blk + 1, n_blk), sub),
        (blk, lax.rem(sub + n_sub - 1, n_sub)),
        (blk, lax.rem(sub + 1, n_sub)),
    ]
    barrier = pltpu.get_barrier_semaphore()
    for face in ENTRY:
        pl.semaphore_signal(barrier, inc=1, device_id=across[face ^ 1], device_id_type=MESH)
    low = -(-plane // 128) * 128
    high = plane * last // 128 * 128
    piece = lambda a, b: (fields_hbm.at[:, 0, a:b], fields_ref.at[:, a:b])
    pairs = [
        piece(0, low), piece(high, points), piece(low, high),
        (pick_hbm, pick_ref), (fwd_hbm, fwd_ref), (lane_hbm, lane_ref), (back_hbm, back_ref),
        (flux_hbm, flux_ref), (deriv_hbm, deriv_ref), (put_hbm, put_ref),
        (jac_hbm, jac_ref), (code_hbm, code_ref), (order_hbm, order_ref),
    ]
    loads = [pltpu.make_async_copy(a, b, load_sem.at[i]) for i, (a, b) in enumerate(pairs)]
    for load in loads[:FIRST]:
        load.start()
    copies = [
        pltpu.make_async_remote_copy(
            src_ref=own.at[face],
            dst_ref=remote.at[face ^ 1],
            send_sem=send_sem.at[face],
            recv_sem=recv_sem.at[face ^ 1],
            device_id=across[face],
            device_id_type=MESH,
        )
        for face in range(4)
    ]

    def padded(value):
        return jnp.pad(value, ((0, ROWS - value.shape[0]), (0, LANES - value.shape[1])))

    def slab(i):
        return padded(fields_ref[:, plane * i : plane * (i + 1)])

    lift = 0.5 * last * last * 0.5

    def traces():
        loads[2].wait()
        for face in (2, 3):
            at = (face - 2) * (plane - n)
            runs = [fields_ref[:, plane * i + at : plane * i + at + n] for i in range(n)]
            own[face] = padded(jnp.concatenate(runs, axis=1)).astype(BF)
        for i in range(n):
            xs[i], xl[i] = split(slab(i))
        loads[3].wait()
        stack = xs[...].reshape(n * ROWS, LANES)[:, :plane]
        ends = dot(stack, pick_ref[...]).reshape(n, ROWS, 128)
        for face in (4, 5):
            at = (face - 4) * n
            runs = [ends[i, :, at : at + n] for i in range(n)]
            own[face] = padded(jnp.concatenate(runs, axis=1)).astype(BF)

    def thirds(value):
        lane = lax.broadcasted_iota(jnp.int32, value.shape, value.ndim - 1)
        hi = value.astype(BF).astype(F32)
        return jnp.where(lane < 2 * ROWS, hi, value - hi).astype(BF)

    def volume_flux():
        for load in loads[4:]:
            load.wait()
        raw[...] = jnp.zeros_like(raw)
        for axis in range(3):
            scaled = flux_ref[axis] * (-TIME_STEP * jac_ref[0, axis])
            for k in range(3):
                raw[axis, 0:width, ROWS * k : ROWS * k + width] = scaled
        mix[...] = thirds(raw[...])
        row = lax.broadcasted_iota(jnp.int32, (ROWS, LANES), 0)
        lane = lax.broadcasted_iota(jnp.int32, (ROWS, LANES), 1)
        diagonal = jnp.logical_and(jnp.bitwise_and(lane, ROWS - 1) == row, lane < 3 * ROWS)
        for face in range(6):
            side = lift if face % 2 else -lift
            keep = lift * TIME_STEP * jac_ref[0, face // 2]
            lift_lhs[face] = thirds(raw[face // 2] * side + jnp.where(diagonal, keep, 0.0))
        for i in range(n):
            mixed = fluxed(mix[...].reshape(3 * ROWS, LANES), xs[i], xl[i])
            gx[i] = mixed[:ROWS]
            for axis in range(2):
                part = mixed[ROWS * (axis + 1) : ROWS * (axis + 2)]
                gs[axis, 0, i], gs[axis, 1, i] = split(part)

    def face_facts(face):
        first, second = lane_ref[0:1, :], lane_ref[1:2, :]
        ones = jnp.ones((1, LANES), F32)
        code = code_ref[0, face]
        order = order_ref[0, face].astype(F32)
        swap = jnp.where(code >= 4, 1, 0)
        rev_a = lax.rem(lax.div(code, 2), 2)
        rev_b = lax.rem(code, 2)
        use_first = jnp.where(swap == 1, rev_b, rev_a) == 1
        use_second = jnp.where(swap == 1, rev_a, rev_b) == 1
        sign = jnp.where(use_first, lane_ref[2:3, :], ones) * jnp.where(
            use_second, lane_ref[3:4, :], ones
        )
        keep = jnp.where((first < order) & (second < order), 1.0, 0.0)
        return swap, sign, keep

    def own_faces():
        own_flat = own[...].reshape(6 * ROWS, LANES)[:, :plane]
        own_modes = (dot(own_flat, fwd_ref[0, 0]) + dot(own_flat, fwd_ref[0, 1])).reshape(
            6, ROWS, LANES
        )
        modes = []
        for face in range(6):
            swap, sign, keep = face_facts(face)
            if face < 4:
                modes.append(own_modes[face] * -keep)
            else:
                far = own[face ^ 1][:, :plane]
                turned = dot(far, fwd_ref[swap, 0]) + dot(far, fwd_ref[swap, 1])
                modes.append((turned * sign - own_modes[face]) * keep)
        modes_hi, modes_lo = split(jnp.concatenate(modes, axis=0))
        modes_hi, modes_lo = modes_hi[:, :plane], modes_lo[:, :plane]
        jump = dot(modes_hi, back_ref[0]) + dot(modes_lo, back_ref[0]) + dot(modes_hi, back_ref[1])
        jump_hi, jump_lo = split(jump)
        cut = lambda a, f: a[ROWS * f : ROWS * (f + 1)]
        for face in range(6):
            early[face] = fluxed(lift_lhs[face], cut(jump_hi, face), cut(jump_lo, face))

    def answer(face):
        pl.semaphore_wait(ack.at[face], 1)
        copies[face].start()

    def when(condition, *steps):
        @pl.when(condition)
        def _():
            for step in steps:
                step()

    odd = lax.rem(sub, 2) == 1
    corner = (blk == 0) & (sub < 2)
    even = jnp.logical_not(odd)
    rest = jnp.logical_not(corner)
    y_first = odd | (blk == 0)
    before = odd | corner
    inner = (blk != 0) & (sub != 0)

    loads[0].wait()
    loads[1].wait()
    own[0] = slab(0).astype(BF)
    own[1] = slab(last).astype(BF)
    for load in loads[FIRST:]:
        load.start()
    when(before, traces)
    when(corner, volume_flux, own_faces)
    pl.semaphore_wait(barrier, 2)
    copies[1].start()
    for face in ENTRY:
        pl.semaphore_signal(ack.at[face ^ 1], inc=1, device_id=across[face], device_id_type=MESH)
    when(jnp.logical_not(before), traces)
    copies[3].start()
    when(rest & y_first, lambda: answer(2))
    when(rest & jnp.logical_not(y_first), lambda: answer(0))
    when(rest, volume_flux)
    when(inner & odd, lambda: answer(0))
    when(inner & even, lambda: answer(2))
    when(rest, own_faces)

    for face in range(4):
        swap, sign, keep = face_facts(face)
        scale = sign * keep
        f_hi = (fwd_ref[swap, 0].astype(F32) * scale).astype(BF)[:, :plane]
        f_lo = (fwd_ref[swap, 1].astype(F32) * scale).astype(BF)[:, :plane]
        whole = dot(f_hi, back_ref[0]) + dot(f_lo, back_ref[0]) + dot(f_hi, back_ref[1])
        oper[face, 0], oper[face, 1] = split(whole)

    runs = []
    for i in range(n):
        both = jnp.concatenate([early[f, :, n * i : n * (i + 1)] for f in (4, 5)], axis=1)
        hi = both.astype(BF).astype(F32)
        runs.append(jnp.concatenate([hi, both - hi], axis=1).astype(BF))
    total = dot(jnp.concatenate(runs, axis=0), put_ref[...])
    for axis in range(2):
        hi = gs[axis, 0].reshape(n * ROWS, LANES)[:, :plane]
        lo = gs[axis, 1].reshape(n * ROWS, LANES)[:, :plane]
        total = total + dot(hi, deriv_ref[axis, 0])
        total = total + dot(lo, deriv_ref[axis, 0])
        total = total + dot(hi, deriv_ref[axis, 1])
    vol[...] = total.reshape(n, ROWS, LANES)
    when(corner | ((blk != 0) & (sub == 0)), lambda: answer(2))

    half = n // 2
    for r in range(0, -(-width // 8) * 8, 8):
        for c in range(0, LANES, 128):
            at = (slice(r, r + 8), slice(c, c + 128))
            plus, minus = [], []
            for a in range(half):
                one, two = gx[(a,) + at], gx[(last - a,) + at]
                plus.append(one + two)
                minus.append(one - two)
            middle = gx[(half,) + at]
            for i in range(half):
                even = minus[0] * float(0.5 * (diff[i, 0] - diff[i, last]))
                uneven = middle * float(diff[i, half])
                for a in range(half):
                    uneven = uneven + plus[a] * float(0.5 * (diff[i, a] + diff[i, last - a]))
                    if a:
                        even = even + minus[a] * float(0.5 * (diff[i, a] - diff[i, last - a]))
                vol[(i,) + at] += even + uneven
                vol[(last - i,) + at] += even - uneven
            even = minus[0] * float(diff[half, 0])
            for a in range(1, half):
                even = even + minus[a] * float(diff[half, a])
            vol[(half,) + at] += even
    for i in range(n):
        value = vol[i]
        if i == 0:
            value = value + early[0]
        if i == last:
            value = value + early[1]
        out_ref[:, plane * i : plane * (i + 1)] = value[:width, :plane]
    when(blk == 0, lambda: answer(0))

    def arrived(pair):
        for face in pair:
            copies[face ^ 1].wait_recv()
        return far_terms(pair, remote, oper, lift_lhs)

    for face, part in zip((2, 3), arrived((2, 3))):
        total = (part + early[face])[:width]
        at = (face - 2) * (plane - n)
        for i in range(n):
            out_ref[:, plane * i + at : plane * i + at + n] += total[:, n * i : n * (i + 1)]
    for face in (0, 1):
        copies[face ^ 1].wait_recv()
        far_ref[face] = remote[face]
    for copy in copies:
        copy.wait_send()


def finish(n, part_ref, far_ref, oper, lift_lhs, out_ref, low_ref, high_ref, sem):
    width, points = part_ref.shape
    plane = n * n
    low = low_ref.shape[1]
    high = points - high_ref.shape[1]
    write = lambda a, i, start, stop: pltpu.make_async_copy(
        a, out_ref.at[:, 0, start:stop], sem.at[i]
    )
    inner = write(part_ref.at[:, low:high], 0, low, high)
    inner.start()
    first, second = far_terms((0, 1), far_ref, oper, lift_lhs)
    low_ref[...] = part_ref[:, :low]
    low_ref[:, :plane] += first[:width, :plane]
    high_ref[...] = part_ref[:, high:]
    high_ref[:, points - plane - high :] += second[:width, :plane]
    outer = [write(low_ref, 1, 0, low), write(high_ref, 2, high, points)]
    for copy in outer:
        copy.start()
    for copy in [inner] + outer:
        copy.wait()


def solution(mesh):
    sizes = (mesh.shape["blk"], mesh.shape["sub"])

    def on_device(fields, flux_matrix, inv_jacobian, neighbour, orientation, face_order):
        width, points = fields.shape[1:]
        n = round(points ** (1.0 / 3.0))
        plane = n * n
        *constants, diff = tables(n)
        rows = jnp.transpose(fields, (1, 0, 2))
        hbm = pl.BlockSpec(memory_space=pltpu.HBM)
        operands = [orientation, face_order, inv_jacobian, rows, flux_matrix]
        operands += [jnp.asarray(a) for a in constants]
        vmem = lambda a: pltpu.VMEM(a.shape, a.dtype)
        vmem_spec = pl.BlockSpec(memory_space=pltpu.VMEM)

        def scoped(*refs):
            pl.run_scoped(
                functools.partial(body, n, diff, sizes, *refs),
                pltpu.SemaphoreType.DMA((13,)),
                pltpu.SemaphoreType.DMA((4,)),
                pltpu.SemaphoreType.DMA((4,)),
                pltpu.SemaphoreType.REGULAR((4,)),
            )

        parts = pl.pallas_call(
            scoped,
            out_shape=(
                pltpu.VMEM((width, points), F32),
                pltpu.VMEM((2, ROWS, LANES), BF),
                pltpu.VMEM((4, 2, plane, LANES), BF),
                pltpu.VMEM((6, ROWS, LANES), BF),
            ),
            in_specs=[hbm] * len(operands),
            out_specs=[vmem_spec] * 4,
            scratch_shapes=[pltpu.SMEM(a.shape, a.dtype) for a in operands[:3]]
            + [pltpu.VMEM((width, points), F32)]
            + [vmem(a) for a in operands[4:]]
            + [
                pltpu.VMEM((n, ROWS, LANES), BF),
                pltpu.VMEM((n, ROWS, LANES), BF),
                pltpu.VMEM((n, ROWS, LANES), F32),
                pltpu.VMEM((2, 2, n, ROWS, LANES), BF),
                pltpu.VMEM((n, ROWS, LANES), F32),
                pltpu.VMEM((6, ROWS, LANES), BF),
                pltpu.VMEM((4, ROWS, LANES), BF),
                pltpu.VMEM((3, ROWS, LANES), F32),
                pltpu.VMEM((3, ROWS, LANES), BF),
                pltpu.VMEM((6, ROWS, LANES), F32),
            ],
            compiler_params=pltpu.CompilerParams(
                collective_id=0, has_side_effects=True, vmem_limit_bytes=48 * 1024 * 1024
            ),
        )(*[pltpu.with_memory_space_constraint(a, pltpu.HBM) for a in operands])
        low = -(-plane // 128) * 128
        high = plane * (n - 1) // 128 * 128
        out = pl.pallas_call(
            lambda *refs: pl.run_scoped(
                functools.partial(finish, n, *refs), pltpu.SemaphoreType.DMA((3,))
            ),
            out_shape=jax.ShapeDtypeStruct(rows.shape, F32),
            in_specs=[vmem_spec] * 4,
            out_specs=hbm,
            scratch_shapes=[
                pltpu.VMEM((width, low), F32),
                pltpu.VMEM((width, points - high), F32),
            ],
            compiler_params=pltpu.CompilerParams(vmem_limit_bytes=16 * 1024 * 1024),
        )(*parts)
        return jnp.transpose(out, (1, 0, 2))

    return jax.shard_map(
        on_device,
        mesh=mesh,
        in_specs=(
            P(("blk", "sub"), None, None),
            P(),
            P(("blk", "sub"), None),
            P(("blk", "sub"), None),
            P(("blk", "sub"), None),
            P(("blk", "sub"), None),
        ),
        out_specs=P(("blk", "sub"), None, None),
        check_vma=False,
    )
```

time: 10.8 us -> 9.65 us (0.89)
  Pallas kernels: 10.7 us -> 9.51 us
    pallas_call x2, Pallas kernels: 10.7 us -> 9.51 us  [the longest x1 8.44 us: on_device(): pl.pallas_call(scoped, out_shape=(pltpu.VMEM((width, points), F32), pltpu...]
where the time goes in v3:
time: 9.65 us; the launch traced here: 9.51 us
  Pallas kernels  9.51 us (99%)
    pallas_call x1, Pallas kernels, on_device(): pl.pallas_call(scoped, out_shape=(pltpu.VMEM((width, points), F32), pltpu...  8.44 us
    pallas_call x1, Pallas kernels, on_device(): pl.pallas_call(lambda *refs: pl.run_scoped(functools.partial(finish, n, *...  1.07 us

profile of v3, /device:TPU:0, one launch (start us, length us, event | category | flops | bytes accessed | tf_op | source)
XLA Modules:
  0.0 9.5 jit_solution(11256420086418371192)
XLA Ops:
  0.0 8.4 %shard_map.109 = (f32[55,2197]{1,0:T(8,128)S(1)}, bf16[2,64,256]{2,1,0:T(8,128)(2,1)S(1)}, bf16[4,2,169,256]{3,2,1,0:T(8,128)(2,1)S(1)}, bf16[6,64,256]{2,1,0:T(8,128)(2,1)S(1)}) custom-call(s32[1,6]{1,0:T(1,128)} %refs_0_.1, s32[1,6]{1,0:T(1,128)} %refs_1_.1, f32[1,3]{1,0:T(1,128)} %refs_2_.1, f32[55,1,2197]{2,1,0:T(1,128)} %bitcast.2, ...), custom_call_target="tpu_custom_call" | custom-call | tf_op jit(solution)/shard_map/pallas_call | solution.py:389
  8.4 1.1 %shard_map.110 = f32[55,1,2197]{2,1,0:T(1,128)} custom-call(f32[55,2197]{1,0:T(8,128)S(1)} %get-tuple-element.9.refs_0_, bf16[2,64,256]{2,1,0:T(8,128)(2,1)S(1)} %get-tuple-element.10.refs_1_, bf16[4,2,169,256]{3,2,1,0:T(8,128)(2,1)S(1)} %get-tuple-element.11.refs_2_, bf16[6,64,256]{2,1,0:T(8,128)(2,1)S(1)} %get-tuple-element.12.refs_3_), custom_call_target="tpu_custom_call" | custom-call | tf_op jit(solution)/shard_map/pallas_call | solution.py:420

commit v4 on v3

--- a/solution.py
+++ b/solution.py
@@ -127,10 +127,13 @@
     loads = [pltpu.make_async_copy(a, b, load_sem.at[i]) for i, (a, b) in enumerate(pairs)]
     for load in loads[:FIRST]:
         load.start()
+    used = -(-width // 8) * 8
+    for face in range(4):
+        remote[face, used:] = jnp.zeros((ROWS - used, LANES), BF)
     copies = [
         pltpu.make_async_remote_copy(
-            src_ref=own.at[face],
-            dst_ref=remote.at[face ^ 1],
+            src_ref=own.at[face, 0:used],
+            dst_ref=remote.at[face ^ 1, 0:used],
             send_sem=send_sem.at[face],
             recv_sem=recv_sem.at[face ^ 1],
             device_id=across[face],
@@ -256,7 +259,7 @@
     when(before, traces)
     when(corner, volume_flux, own_faces)
     pl.semaphore_wait(barrier, 2)
-    copies[1].start()
+    when(even | corner, copies[1].start)
     for face in ENTRY:
         pl.semaphore_signal(ack.at[face ^ 1], inc=1, device_id=across[face], device_id_type=MESH)
     when(jnp.logical_not(before), traces)
@@ -264,9 +267,11 @@
     when(rest & y_first, lambda: answer(2))
     when(rest & jnp.logical_not(y_first), lambda: answer(0))
     when(rest, volume_flux)
+    when(odd & rest, copies[1].start)
     when(inner & odd, lambda: answer(0))
     when(inner & even, lambda: answer(2))
     when(rest, own_faces)
+    when((blk != 0) & (sub == 0), lambda: answer(2))
 
     for face in range(4):
         swap, sign, keep = face_facts(face)
@@ -289,7 +294,8 @@
         total = total + dot(lo, deriv_ref[axis, 0])
         total = total + dot(hi, deriv_ref[axis, 1])
     vol[...] = total.reshape(n, ROWS, LANES)
-    when(corner | ((blk != 0) & (sub == 0)), lambda: answer(2))
+    when(corner, lambda: answer(2))
+    when(rest & (blk == 0), lambda: answer(0))
 
     half = n // 2
     for r in range(0, -(-width // 8) * 8, 8):
@@ -321,7 +327,7 @@
         if i == last:
             value = value + early[1]
         out_ref[:, plane * i : plane * (i + 1)] = value[:width, :plane]
-    when(blk == 0, lambda: answer(0))
+    when(corner, lambda: answer(0))
 
     def arrived(pair):
         for face in pair:

time: 9.65 us -> 9.29 us (0.963)
  Pallas kernels: 9.51 us -> 9.15 us
    pallas_call x1, Pallas kernels: 8.44 us -> 8.08 us  [on_device(): pl.pallas_call(scoped, out_shape=(pltpu.VMEM((width, points), F32), pltpu...]
where the time goes in v4:
time: 9.29 us; the launch traced here: 9.15 us
  Pallas kernels  9.15 us (98%)
    pallas_call x1, Pallas kernels, on_device(): pl.pallas_call(scoped, out_shape=(pltpu.VMEM((width, points), F32), pltpu...  8.08 us
    pallas_call x1, Pallas kernels, on_device(): pl.pallas_call(lambda *refs: pl.run_scoped(functools.partial(finish, n, *...  1.07 us

profile of v4, /device:TPU:0, one launch (start us, length us, event | category | flops | bytes accessed | tf_op | source)
XLA Modules:
  0.0 9.2 jit_solution(13192512993571199872)
XLA Ops:
  0.0 8.1 %shard_map.109 = (f32[55,2197]{1,0:T(8,128)S(1)}, bf16[2,64,256]{2,1,0:T(8,128)(2,1)S(1)}, bf16[4,2,169,256]{3,2,1,0:T(8,128)(2,1)S(1)}, bf16[6,64,256]{2,1,0:T(8,128)(2,1)S(1)}) custom-call(s32[1,6]{1,0:T(1,128)} %refs_0_.1, s32[1,6]{1,0:T(1,128)} %refs_1_.1, f32[1,3]{1,0:T(1,128)} %refs_2_.1, f32[55,1,2197]{2,1,0:T(1,128)} %bitcast.2, ...), custom_call_target="tpu_custom_call" | custom-call | tf_op jit(solution)/shard_map/pallas_call | solution.py:395
  8.1 1.1 %shard_map.110 = f32[55,1,2197]{2,1,0:T(1,128)} custom-call(f32[55,2197]{1,0:T(8,128)S(1)} %get-tuple-element.9.refs_0_, bf16[2,64,256]{2,1,0:T(8,128)(2,1)S(1)} %get-tuple-element.10.refs_1_, bf16[4,2,169,256]{3,2,1,0:T(8,128)(2,1)S(1)} %get-tuple-element.11.refs_2_, bf16[6,64,256]{2,1,0:T(8,128)(2,1)S(1)} %get-tuple-element.12.refs_3_), custom_call_target="tpu_custom_call" | custom-call | tf_op jit(solution)/shard_map/pallas_call | solution.py:426

commit v5 on v4

--- a/solution.py
+++ b/solution.py
@@ -15,7 +15,6 @@
 LANES = 256
 TIME_STEP = 0.01
 ENTRY = (1, 3)
-FIRST = 13
 
 
 def cheb_np(n):
@@ -80,14 +79,15 @@
 
 
 def fluxed(lhs, hi, lo):
-    return dot(lhs[:, : 3 * ROWS], jnp.concatenate([hi, lo, hi], axis=0))
-
-
-def far_terms(pair, far, oper, lift_lhs):
-    plane = oper.shape[2]
-    turned = [
-        dot(far[f][:, :plane], oper[f, 0]) + dot(far[f][:, :plane], oper[f, 1]) for f in pair
-    ]
+    return dot(lhs[:, : 3 * ROWS], jnp.concatenate([hi, hi, lo], axis=0))
+
+
+def far_terms(pair, far, oper, lift_lhs, plane):
+    turned = []
+    for f in pair:
+        depth = plane if f > 1 else LANES
+        one = far[f][:, :depth]
+        turned.append(dot(one, oper[f, 0, :depth]) + dot(one, oper[f, 1, :depth]))
     return [fluxed(lift_lhs[f], *split(t)) for f, t in zip(pair, turned)]
 
 
@@ -113,19 +113,20 @@
         (blk, lax.rem(sub + 1, n_sub)),
     ]
     barrier = pltpu.get_barrier_semaphore()
-    for face in ENTRY:
-        pl.semaphore_signal(barrier, inc=1, device_id=across[face ^ 1], device_id_type=MESH)
     low = -(-plane // 128) * 128
     high = plane * last // 128 * 128
     piece = lambda a, b: (fields_hbm.at[:, 0, a:b], fields_ref.at[:, a:b])
     pairs = [
-        piece(0, low), piece(high, points), piece(low, high),
+        piece(high, points), piece(0, low), piece(low, high),
         (pick_hbm, pick_ref), (fwd_hbm, fwd_ref), (lane_hbm, lane_ref), (back_hbm, back_ref),
         (flux_hbm, flux_ref), (deriv_hbm, deriv_ref), (put_hbm, put_ref),
         (jac_hbm, jac_ref), (code_hbm, code_ref), (order_hbm, order_ref),
     ]
     loads = [pltpu.make_async_copy(a, b, load_sem.at[i]) for i, (a, b) in enumerate(pairs)]
-    for load in loads[:FIRST]:
+    loads[0].start()
+    for face in ENTRY:
+        pl.semaphore_signal(barrier, inc=1, device_id=across[face ^ 1], device_id_type=MESH)
+    for load in loads[1:]:
         load.start()
     used = -(-width // 8) * 8
     for face in range(4):
@@ -151,6 +152,8 @@
     lift = 0.5 * last * last * 0.5
 
     def traces():
+        loads[1].wait()
+        own[0] = slab(0).astype(BF)
         loads[2].wait()
         for face in (2, 3):
             at = (face - 2) * (plane - n)
@@ -171,7 +174,13 @@
         hi = value.astype(BF).astype(F32)
         return jnp.where(lane < 2 * ROWS, hi, value - hi).astype(BF)
 
-    def volume_flux():
+    def thirds(value):
+        hi = value.astype(BF).astype(F32)
+        lane = lax.broadcasted_iota(jnp.int32, value.shape, value.ndim - 1)
+        lows = (lane >= ROWS) & (lane < 2 * ROWS)
+        return jnp.where(lows, value - hi, hi).astype(BF)
+
+    def flux_matrices():
         for load in loads[4:]:
             load.wait()
         raw[...] = jnp.zeros_like(raw)
@@ -182,11 +191,13 @@
         mix[...] = thirds(raw[...])
         row = lax.broadcasted_iota(jnp.int32, (ROWS, LANES), 0)
         lane = lax.broadcasted_iota(jnp.int32, (ROWS, LANES), 1)
-        diagonal = jnp.logical_and(jnp.bitwise_and(lane, ROWS - 1) == row, lane < 3 * ROWS)
+        diagonal = (jnp.bitwise_and(lane, ROWS - 1) == row) & (lane < 3 * ROWS)
         for face in range(6):
             side = lift if face % 2 else -lift
             keep = lift * TIME_STEP * jac_ref[0, face // 2]
             lift_lhs[face] = thirds(raw[face // 2] * side + jnp.where(diagonal, keep, 0.0))
+
+    def volume_flux():
         for i in range(n):
             mixed = fluxed(mix[...].reshape(3 * ROWS, LANES), xs[i], xl[i])
             gx[i] = mixed[:ROWS]
@@ -211,7 +222,8 @@
         return swap, sign, keep
 
     def own_faces():
-        own_flat = own[...].reshape(6 * ROWS, LANES)[:, :plane]
+        rest_flat = own[2:].reshape(4 * ROWS, LANES)
+        own_flat = jnp.concatenate([xs[0], xs[last], rest_flat], axis=0)[:, :plane]
         own_modes = (dot(own_flat, fwd_ref[0, 0]) + dot(own_flat, fwd_ref[0, 1])).reshape(
             6, ROWS, LANES
         )
@@ -251,13 +263,15 @@
     inner = (blk != 0) & (sub != 0)
 
     loads[0].wait()
-    loads[1].wait()
-    own[0] = slab(0).astype(BF)
-    own[1] = slab(last).astype(BF)
-    for load in loads[FIRST:]:
-        load.start()
+    offset = plane * last - high
+    tail = points - high - LANES
+    lane = lax.broadcasted_iota(jnp.int32, (width, 128), 1)
+    ahead = jnp.pad(fields_ref[:, high + LANES :], ((0, 0), (0, 128 - tail)))
+    merged = jnp.where(lane < tail, ahead, fields_ref[:, high : high + 128])
+    turned = jnp.concatenate([merged, fields_ref[:, high + 128 : high + LANES]], axis=1)
+    own[1] = padded(turned).astype(BF)
     when(before, traces)
-    when(corner, volume_flux, own_faces)
+    when(corner, flux_matrices, volume_flux, own_faces)
     pl.semaphore_wait(barrier, 2)
     when(even | corner, copies[1].start)
     for face in ENTRY:
@@ -266,8 +280,9 @@
     copies[3].start()
     when(rest & y_first, lambda: answer(2))
     when(rest & jnp.logical_not(y_first), lambda: answer(0))
+    when(rest, flux_matrices)
+    when(odd & rest, copies[1].start)
     when(rest, volume_flux)
-    when(odd & rest, copies[1].start)
     when(inner & odd, lambda: answer(0))
     when(inner & even, lambda: answer(2))
     when(rest, own_faces)
@@ -279,7 +294,17 @@
         f_hi = (fwd_ref[swap, 0].astype(F32) * scale).astype(BF)[:, :plane]
         f_lo = (fwd_ref[swap, 1].astype(F32) * scale).astype(BF)[:, :plane]
         whole = dot(f_hi, back_ref[0]) + dot(f_lo, back_ref[0]) + dot(f_hi, back_ref[1])
+        if face == 1:
+            whole = pltpu.roll(whole, offset, 1)
+        zeros = jnp.zeros((LANES - plane, LANES), F32)
+        if face == 0:
+            head = plane - tail
+            whole = jnp.concatenate([whole[head:], zeros, whole[:head]], axis=0)
+        else:
+            whole = jnp.concatenate([whole, zeros], axis=0)
         oper[face, 0], oper[face, 1] = split(whole)
+
+    when(rest & even & (blk == 0), lambda: answer(0))
 
     runs = []
     for i in range(n):
@@ -295,7 +320,7 @@
         total = total + dot(hi, deriv_ref[axis, 1])
     vol[...] = total.reshape(n, ROWS, LANES)
     when(corner, lambda: answer(2))
-    when(rest & (blk == 0), lambda: answer(0))
+    when(rest & odd & (blk == 0), lambda: answer(0))
 
     half = n // 2
     for r in range(0, -(-width // 8) * 8, 8):
@@ -332,7 +357,7 @@
     def arrived(pair):
         for face in pair:
             copies[face ^ 1].wait_recv()
-        return far_terms(pair, remote, oper, lift_lhs)
+        return far_terms(pair, remote, oper, lift_lhs, plane)
 
     for face, part in zip((2, 3), arrived((2, 3))):
         total = (part + early[face])[:width]
@@ -356,11 +381,14 @@
     )
     inner = write(part_ref.at[:, low:high], 0, low, high)
     inner.start()
-    first, second = far_terms((0, 1), far_ref, oper, lift_lhs)
-    low_ref[...] = part_ref[:, :low]
-    low_ref[:, :plane] += first[:width, :plane]
-    high_ref[...] = part_ref[:, high:]
-    high_ref[:, points - plane - high :] += second[:width, :plane]
+    first, second = (part[:width] for part in far_terms((0, 1), far_ref, oper, lift_lhs, plane))
+    low_ref[...] = part_ref[:, :low] + first[:, :low]
+    lane = lax.broadcasted_iota(jnp.int32, (width, 128), 1)
+    begun = jnp.where(lane >= points - plane - high, second[:, :128], 0.0)
+    high_ref[:, :128] = part_ref[:, high : high + 128] + begun
+    high_ref[:, 128:LANES] = part_ref[:, high + 128 : high + LANES] + second[:, 128:]
+    tail = points - high - LANES
+    high_ref[:, LANES:] = part_ref[:, high + LANES :] + second[:, :tail]
     outer = [write(low_ref, 1, 0, low), write(high_ref, 2, high, points)]
     for copy in outer:
         copy.start()
@@ -397,7 +425,7 @@
             out_shape=(
                 pltpu.VMEM((width, points), F32),
                 pltpu.VMEM((2, ROWS, LANES), BF),
-                pltpu.VMEM((4, 2, plane, LANES), BF),
+                pltpu.VMEM((4, 2, LANES, LANES), BF),
                 pltpu.VMEM((6, ROWS, LANES), BF),
             ),
             in_specs=[hbm] * len(operands),

time: 9.29 us -> 9.03 us (0.972)
  Pallas kernels: 9.15 us -> 8.89 us
    pallas_call x1, Pallas kernels: 8.08 us -> 7.85 us  [on_device(): pl.pallas_call(scoped, out_shape=(pltpu.VMEM((width, points), F32), pltpu...]
where the time goes in v5:
time: 9.03 us; the launch traced here: 8.89 us
  Pallas kernels  8.89 us (98%)
    pallas_call x1, Pallas kernels, on_device(): pl.pallas_call(scoped, out_shape=(pltpu.VMEM((width, points), F32), pltpu...  7.85 us
    pallas_call x1, Pallas kernels, on_device(): pl.pallas_call(lambda *refs: pl.run_scoped(functools.partial(finish, n, *...  1.03 us

profile of v5, /device:TPU:0, one launch (start us, length us, event | category | flops | bytes accessed | tf_op | source)
XLA Modules:
  0.0 8.9 jit_solution(11825262351985343117)
XLA Ops:
  0.0 7.9 %shard_map.109 = (f32[55,2197]{1,0:T(8,128)S(1)}, bf16[2,64,256]{2,1,0:T(8,128)(2,1)S(1)}, bf16[4,2,256,256]{3,2,1,0:T(8,128)(2,1)S(1)}, bf16[6,64,256]{2,1,0:T(8,128)(2,1)S(1)}) custom-call(s32[1,6]{1,0:T(1,128)} %refs_0_.1, s32[1,6]{1,0:T(1,128)} %refs_1_.1, f32[1,3]{1,0:T(1,128)} %refs_2_.1, f32[55,1,2197]{2,1,0:T(1,128)} %bitcast.2, ...), custom_call_target="tpu_custom_call" | custom-call | tf_op jit(solution)/shard_map/pallas_call | solution.py:423
  7.9 1.0 %shard_map.110 = f32[55,1,2197]{2,1,0:T(1,128)} custom-call(f32[55,2197]{1,0:T(8,128)S(1)} %get-tuple-element.9.refs_0_, bf16[2,64,256]{2,1,0:T(8,128)(2,1)S(1)} %get-tuple-element.10.refs_1_, bf16[4,2,256,256]{3,2,1,0:T(8,128)(2,1)S(1)} %get-tuple-element.11.refs_2_, bf16[6,64,256]{2,1,0:T(8,128)(2,1)S(1)} %get-tuple-element.12.refs_3_), custom_call_target="tpu_custom_call" | custom-call | tf_op jit(solution)/shard_map/pallas_call | solution.py:454

commit v6 on v5

--- a/solution.py
+++ b/solution.py
@@ -82,13 +82,13 @@
     return dot(lhs[:, : 3 * ROWS], jnp.concatenate([hi, hi, lo], axis=0))
 
 
-def far_terms(pair, far, oper, lift_lhs, plane):
+def far_terms(faces, far, oper, lift_lhs, plane):
     turned = []
-    for f in pair:
-        depth = plane if f > 1 else LANES
-        one = far[f][:, :depth]
+    for f in faces:
+        depth = plane if f else LANES
+        one = far(f)[:, :depth]
         turned.append(dot(one, oper[f, 0, :depth]) + dot(one, oper[f, 1, :depth]))
-    return [fluxed(lift_lhs[f], *split(t)) for f, t in zip(pair, turned)]
+    return [fluxed(lift_lhs[f], *split(t)) for f, t in zip(faces, turned)]
 
 
 def body(
@@ -129,12 +129,13 @@
     for load in loads[1:]:
         load.start()
     used = -(-width // 8) * 8
-    for face in range(4):
+    far_ref[used:] = jnp.zeros((ROWS - used, LANES), BF)
+    for face in range(1, 4):
         remote[face, used:] = jnp.zeros((ROWS - used, LANES), BF)
     copies = [
         pltpu.make_async_remote_copy(
             src_ref=own.at[face, 0:used],
-            dst_ref=remote.at[face ^ 1, 0:used],
+            dst_ref=far_ref.at[0:used] if face == 1 else remote.at[face ^ 1, 0:used],
             send_sem=send_sem.at[face],
             recv_sem=recv_sem.at[face ^ 1],
             device_id=across[face],
@@ -259,7 +260,7 @@
     even = jnp.logical_not(odd)
     rest = jnp.logical_not(corner)
     y_first = odd | (blk == 0)
-    before = odd | corner
+    before = odd | (blk != n_blk - 1)
     inner = (blk != 0) & (sub != 0)
 
     loads[0].wait()
@@ -271,7 +272,7 @@
     turned = jnp.concatenate([merged, fields_ref[:, high + 128 : high + LANES]], axis=1)
     own[1] = padded(turned).astype(BF)
     when(before, traces)
-    when(corner, flux_matrices, volume_flux, own_faces)
+    when(corner, flux_matrices, volume_flux)
     pl.semaphore_wait(barrier, 2)
     when(even | corner, copies[1].start)
     for face in ENTRY:
@@ -285,7 +286,7 @@
     when(rest, volume_flux)
     when(inner & odd, lambda: answer(0))
     when(inner & even, lambda: answer(2))
-    when(rest, own_faces)
+    own_faces()
     when((blk != 0) & (sub == 0), lambda: answer(2))
 
     for face in range(4):
@@ -354,46 +355,44 @@
         out_ref[:, plane * i : plane * (i + 1)] = value[:width, :plane]
     when(corner, lambda: answer(0))
 
-    def arrived(pair):
-        for face in pair:
+    def arrived(*faces):
+        for face in faces:
             copies[face ^ 1].wait_recv()
-        return far_terms(pair, remote, oper, lift_lhs, plane)
-
-    for face, part in zip((2, 3), arrived((2, 3))):
-        total = (part + early[face])[:width]
-        at = (face - 2) * (plane - n)
-        for i in range(n):
-            out_ref[:, plane * i + at : plane * i + at + n] += total[:, n * i : n * (i + 1)]
-    for face in (0, 1):
-        copies[face ^ 1].wait_recv()
-        far_ref[face] = remote[face]
+        terms = far_terms(faces, lambda f: remote[f], oper, lift_lhs, plane)
+        for face, part in zip(faces, terms):
+            if face == 1:
+                part = part[:width]
+                begun = jnp.where(lane >= offset, part[:, :128], 0.0)
+                out_ref[:, high : high + 128] += begun
+                out_ref[:, high + 128 : high + LANES] += part[:, 128:]
+                out_ref[:, high + LANES :] += part[:, :tail]
+                continue
+            total = (part + early[face])[:width]
+            at = (face - 2) * (plane - n)
+            for i in range(n):
+                out_ref[:, plane * i + at : plane * i + at + n] += total[:, n * i : n * (i + 1)]
+
+    arrived(2, 3)
+    arrived(1)
+    copies[1].wait_recv()
     for copy in copies:
         copy.wait_send()
 
 
-def finish(n, part_ref, far_ref, oper, lift_lhs, out_ref, low_ref, high_ref, sem):
+def finish(n, part_ref, far_ref, oper, lift_lhs, out_ref, low_ref, sem):
     width, points = part_ref.shape
-    plane = n * n
     low = low_ref.shape[1]
-    high = points - high_ref.shape[1]
     write = lambda a, i, start, stop: pltpu.make_async_copy(
         a, out_ref.at[:, 0, start:stop], sem.at[i]
     )
-    inner = write(part_ref.at[:, low:high], 0, low, high)
+    inner = write(part_ref.at[:, low:], 0, low, points)
     inner.start()
-    first, second = (part[:width] for part in far_terms((0, 1), far_ref, oper, lift_lhs, plane))
-    low_ref[...] = part_ref[:, :low] + first[:, :low]
-    lane = lax.broadcasted_iota(jnp.int32, (width, 128), 1)
-    begun = jnp.where(lane >= points - plane - high, second[:, :128], 0.0)
-    high_ref[:, :128] = part_ref[:, high : high + 128] + begun
-    high_ref[:, 128:LANES] = part_ref[:, high + 128 : high + LANES] + second[:, 128:]
-    tail = points - high - LANES
-    high_ref[:, LANES:] = part_ref[:, high + LANES :] + second[:, :tail]
-    outer = [write(low_ref, 1, 0, low), write(high_ref, 2, high, points)]
-    for copy in outer:
-        copy.start()
-    for copy in [inner] + outer:
-        copy.wait()
+    (term,) = far_terms((0,), lambda f: far_ref[...], oper, lift_lhs, n * n)
+    low_ref[...] = part_ref[:, :low] + term[:width, :low]
+    outer = write(low_ref, 1, 0, low)
+    outer.start()
+    inner.wait()
+    outer.wait()
 
 
 def solution(mesh):
@@ -424,7 +423,7 @@
             scoped,
             out_shape=(
                 pltpu.VMEM((width, points), F32),
-                pltpu.VMEM((2, ROWS, LANES), BF),
+                pltpu.VMEM((ROWS, LANES), BF),
                 pltpu.VMEM((4, 2, LANES, LANES), BF),
                 pltpu.VMEM((6, ROWS, LANES), BF),
             ),
@@ -450,17 +449,15 @@
             ),
         )(*[pltpu.with_memory_space_constraint(a, pltpu.HBM) for a in operands])
         low = -(-plane // 128) * 128
-        high = plane * (n - 1) // 128 * 128
         out = pl.pallas_call(
             lambda *refs: pl.run_scoped(
-                functools.partial(finish, n, *refs), pltpu.SemaphoreType.DMA((3,))
+                functools.partial(finish, n, *refs), pltpu.SemaphoreType.DMA((2,))
             ),
             out_shape=jax.ShapeDtypeStruct(rows.shape, F32),
             in_specs=[vmem_spec] * 4,
             out_specs=hbm,
             scratch_shapes=[
                 pltpu.VMEM((width, low), F32),
-                pltpu.VMEM((width, points - high), F32),
             ],
             compiler_params=pltpu.CompilerParams(vmem_limit_bytes=16 * 1024 * 1024),
         )(*parts)

time: 9.03 us -> 8.91 us (0.987)
  Pallas kernels: 8.89 us -> 8.77 us
    pallas_call x1, Pallas kernels: 1.03 us -> 0.94 us  [on_device(): pl.pallas_call(lambda *refs: pl.run_scoped(functools.partial(finish, n, *...]
where the time goes in v6:
time: 8.91 us; the launch traced here: 8.77 us
  Pallas kernels  8.77 us (98%)
    pallas_call x1, Pallas kernels, on_device(): pl.pallas_call(scoped, out_shape=(pltpu.VMEM((width, points), F32), pltpu...  7.84 us
    pallas_call x1, Pallas kernels, on_device(): pl.pallas_call(lambda *refs: pl.run_scoped(functools.partial(finish, n, *...  0.94 us

profile of v6, /device:TPU:0, one launch (start us, length us, event | category | flops | bytes accessed | tf_op | source)
XLA Modules:
  0.0 8.8 jit_solution(8552263709128501621)
XLA Ops:
  0.0 7.8 %shard_map.109 = (f32[55,2197]{1,0:T(8,128)S(1)}, bf16[64,256]{1,0:T(8,128)(2,1)S(1)}, bf16[4,2,256,256]{3,2,1,0:T(8,128)(2,1)S(1)}, bf16[6,64,256]{2,1,0:T(8,128)(2,1)S(1)}) custom-call(s32[1,6]{1,0:T(1,128)} %refs_0_.1, s32[1,6]{1,0:T(1,128)} %refs_1_.1, f32[1,3]{1,0:T(1,128)} %refs_2_.1, f32[55,1,2197]{2,1,0:T(1,128)} %bitcast.2, f32[3,55,55]{2,1,0:T(8,128)} %refs_4_.1, ...), custom_call_target="tpu_custom_call" | custom-call | tf_op jit(solution)/shard_map/pallas_call | solution.py:422
  7.8 0.9 %shard_map.110 = f32[55,1,2197]{2,1,0:T(1,128)} custom-call(f32[55,2197]{1,0:T(8,128)S(1)} %get-tuple-element.9.refs_0_, bf16[64,256]{1,0:T(8,128)(2,1)S(1)} %get-tuple-element.10.refs_1_, bf16[4,2,256,256]{3,2,1,0:T(8,128)(2,1)S(1)} %get-tuple-element.11.refs_2_, bf16[6,64,256]{2,1,0:T(8,128)(2,1)S(1)} %get-tuple-element.12.refs_3_), custom_call_target="tpu_custom_call" | custom-call | tf_op jit(solution)/shard_map/pallas_call | solution.py:452

commit v7 on v6

--- a/solution.py
+++ b/solution.py
@@ -170,16 +170,10 @@
             runs = [ends[i, :, at : at + n] for i in range(n)]
             own[face] = padded(jnp.concatenate(runs, axis=1)).astype(BF)
 
-    def thirds(value):
-        lane = lax.broadcasted_iota(jnp.int32, value.shape, value.ndim - 1)
-        hi = value.astype(BF).astype(F32)
-        return jnp.where(lane < 2 * ROWS, hi, value - hi).astype(BF)
-
-    def thirds(value):
+    def parts(value):
         hi = value.astype(BF).astype(F32)
         lane = lax.broadcasted_iota(jnp.int32, value.shape, value.ndim - 1)
-        lows = (lane >= ROWS) & (lane < 2 * ROWS)
-        return jnp.where(lows, value - hi, hi).astype(BF)
+        return jnp.where(jnp.bitwise_and(lane, ROWS) == 0, hi, value - hi).astype(BF)
 
     def flux_matrices():
         for load in loads[4:]:
@@ -187,20 +181,21 @@
         raw[...] = jnp.zeros_like(raw)
         for axis in range(3):
             scaled = flux_ref[axis] * (-TIME_STEP * jac_ref[0, axis])
-            for k in range(3):
+            for k in range(LANES // ROWS):
                 raw[axis, 0:width, ROWS * k : ROWS * k + width] = scaled
-        mix[...] = thirds(raw[...])
+        mix[...] = parts(raw[...])
         row = lax.broadcasted_iota(jnp.int32, (ROWS, LANES), 0)
         lane = lax.broadcasted_iota(jnp.int32, (ROWS, LANES), 1)
-        diagonal = (jnp.bitwise_and(lane, ROWS - 1) == row) & (lane < 3 * ROWS)
+        diagonal = jnp.bitwise_and(lane, ROWS - 1) == row
         for face in range(6):
             side = lift if face % 2 else -lift
             keep = lift * TIME_STEP * jac_ref[0, face // 2]
-            lift_lhs[face] = thirds(raw[face // 2] * side + jnp.where(diagonal, keep, 0.0))
+            lift_lhs[face] = parts(raw[face // 2] * side + jnp.where(diagonal, keep, 0.0))
 
     def volume_flux():
         for i in range(n):
-            mixed = fluxed(mix[...].reshape(3 * ROWS, LANES), xs[i], xl[i])
+            both = jnp.concatenate([xs[i], xs[i], xl[i], xl[i]], axis=0)
+            mixed = dot(mix[...].reshape(3 * ROWS, LANES), both)
             gx[i] = mixed[:ROWS]
             for axis in range(2):
                 part = mixed[ROWS * (axis + 1) : ROWS * (axis + 2)]
@@ -295,6 +290,7 @@
         f_hi = (fwd_ref[swap, 0].astype(F32) * scale).astype(BF)[:, :plane]
         f_lo = (fwd_ref[swap, 1].astype(F32) * scale).astype(BF)[:, :plane]
         whole = dot(f_hi, back_ref[0]) + dot(f_lo, back_ref[0]) + dot(f_hi, back_ref[1])
+        whole = whole + dot(f_lo, back_ref[1])
         if face == 1:
             whole = pltpu.roll(whole, offset, 1)
         zeros = jnp.zeros((LANES - plane, LANES), F32)
@@ -305,7 +301,7 @@
             whole = jnp.concatenate([whole, zeros], axis=0)
         oper[face, 0], oper[face, 1] = split(whole)
 
-    when(rest & even & (blk == 0), lambda: answer(0))
+    when(rest & (blk == 0), lambda: answer(0))
 
     runs = []
     for i in range(n):
@@ -321,7 +317,6 @@
         total = total + dot(hi, deriv_ref[axis, 1])
     vol[...] = total.reshape(n, ROWS, LANES)
     when(corner, lambda: answer(2))
-    when(rest & odd & (blk == 0), lambda: answer(0))
 
     half = n // 2
     for r in range(0, -(-width // 8) * 8, 8):

time: 8.91 us -> 8.91 us (level)
  no operation moved by 1% of the time
where the time goes in v7:
time: 8.91 us; the launch traced here: 8.77 us
  Pallas kernels  8.77 us (98%)
    pallas_call x1, Pallas kernels, on_device(): pl.pallas_call(scoped, out_shape=(pltpu.VMEM((width, points), F32), pltpu...  7.84 us
    pallas_call x1, Pallas kernels, on_device(): pl.pallas_call(lambda *refs: pl.run_scoped(functools.partial(finish, n, *...  0.94 us

profile of v7, /device:TPU:0, one launch (start us, length us, event | category | flops | bytes accessed | tf_op | source)
XLA Modules:
  0.0 8.8 jit_solution(4015771817608879626)
XLA Ops:
  0.0 7.8 %shard_map.109 = (f32[55,2197]{1,0:T(8,128)S(1)}, bf16[64,256]{1,0:T(8,128)(2,1)S(1)}, bf16[4,2,256,256]{3,2,1,0:T(8,128)(2,1)S(1)}, bf16[6,64,256]{2,1,0:T(8,128)(2,1)S(1)}) custom-call(s32[1,6]{1,0:T(1,128)} %refs_0_.1, s32[1,6]{1,0:T(1,128)} %refs_1_.1, f32[1,3]{1,0:T(1,128)} %refs_2_.1, f32[55,1,2197]{2,1,0:T(1,128)} %bitcast.2, f32[3,55,55]{2,1,0:T(8,128)} %refs_4_.1, ...), custom_call_target="tpu_custom_call" | custom-call | tf_op jit(solution)/shard_map/pallas_call | solution.py:417
  7.8 0.9 %shard_map.110 = f32[55,1,2197]{2,1,0:T(1,128)} custom-call(f32[55,2197]{1,0:T(8,128)S(1)} %get-tuple-element.9.refs_0_, bf16[64,256]{1,0:T(8,128)(2,1)S(1)} %get-tuple-element.10.refs_1_, bf16[4,2,256,256]{3,2,1,0:T(8,128)(2,1)S(1)} %get-tuple-element.11.refs_2_, bf16[6,64,256]{2,1,0:T(8,128)(2,1)S(1)} %get-tuple-element.12.refs_3_), custom_call_target="tpu_custom_call" | custom-call | tf_op jit(solution)/shard_map/pallas_call | solution.py:447

commit v8 on v7

--- a/solution.py
+++ b/solution.py
@@ -15,6 +15,7 @@
 LANES = 256
 TIME_STEP = 0.01
 ENTRY = (1, 3)
+STRIP = 16
 
 
 def cheb_np(n):
@@ -117,16 +118,21 @@
     high = plane * last // 128 * 128
     piece = lambda a, b: (fields_hbm.at[:, 0, a:b], fields_ref.at[:, a:b])
     pairs = [
-        piece(high, points), piece(0, low), piece(low, high),
+        piece(0, low), piece(low, high),
         (pick_hbm, pick_ref), (fwd_hbm, fwd_ref), (lane_hbm, lane_ref), (back_hbm, back_ref),
         (flux_hbm, flux_ref), (deriv_hbm, deriv_ref), (put_hbm, put_ref),
         (jac_hbm, jac_ref), (code_hbm, code_ref), (order_hbm, order_ref),
     ]
+    whole_loads = len(pairs)
+    for r in range(0, width, STRIP):
+        strip = slice(r, min(r + STRIP, width))
+        pairs.append((fields_hbm.at[strip, 0, high:], fields_ref.at[strip, high:]))
     loads = [pltpu.make_async_copy(a, b, load_sem.at[i]) for i, (a, b) in enumerate(pairs)]
-    loads[0].start()
+    for load in loads[whole_loads:]:
+        load.start()
     for face in ENTRY:
         pl.semaphore_signal(barrier, inc=1, device_id=across[face ^ 1], device_id_type=MESH)
-    for load in loads[1:]:
+    for load in loads[:whole_loads]:
         load.start()
     used = -(-width // 8) * 8
     far_ref[used:] = jnp.zeros((ROWS - used, LANES), BF)
@@ -153,16 +159,16 @@
     lift = 0.5 * last * last * 0.5
 
     def traces():
+        loads[0].wait()
+        own[0] = slab(0).astype(BF)
         loads[1].wait()
-        own[0] = slab(0).astype(BF)
-        loads[2].wait()
         for face in (2, 3):
             at = (face - 2) * (plane - n)
             runs = [fields_ref[:, plane * i + at : plane * i + at + n] for i in range(n)]
             own[face] = padded(jnp.concatenate(runs, axis=1)).astype(BF)
         for i in range(n):
             xs[i], xl[i] = split(slab(i))
-        loads[3].wait()
+        loads[2].wait()
         stack = xs[...].reshape(n * ROWS, LANES)[:, :plane]
         ends = dot(stack, pick_ref[...]).reshape(n, ROWS, 128)
         for face in (4, 5):
@@ -176,7 +182,7 @@
         return jnp.where(jnp.bitwise_and(lane, ROWS) == 0, hi, value - hi).astype(BF)
 
     def flux_matrices():
-        for load in loads[4:]:
+        for load in loads[3:whole_loads]:
             load.wait()
         raw[...] = jnp.zeros_like(raw)
         for axis in range(3):
@@ -258,7 +264,8 @@
     before = odd | (blk != n_blk - 1)
     inner = (blk != 0) & (sub != 0)
 
-    loads[0].wait()
+    for load in loads[whole_loads:]:
+        load.wait()
     offset = plane * last - high
     tail = points - high - LANES
     lane = lax.broadcasted_iota(jnp.int32, (width, 128), 1)
@@ -408,7 +415,7 @@
         def scoped(*refs):
             pl.run_scoped(
                 functools.partial(body, n, diff, sizes, *refs),
-                pltpu.SemaphoreType.DMA((13,)),
+                pltpu.SemaphoreType.DMA((len(operands) + 1 + -(-width // STRIP),)),
                 pltpu.SemaphoreType.DMA((4,)),
                 pltpu.SemaphoreType.DMA((4,)),
                 pltpu.SemaphoreType.REGULAR((4,)),

time: 8.91 us -> 8.82 us (0.990)
  Pallas kernels: 8.77 us -> 8.67 us
    pallas_call x1, Pallas kernels: 7.84 us -> 7.72 us  [on_device(): pl.pallas_call(scoped, out_shape=(pltpu.VMEM((width, points), F32), pltpu...]
where the time goes in v8:
time: 8.82 us; the launch traced here: 8.68 us
  Pallas kernels  8.67 us (98%)
    pallas_call x1, Pallas kernels, on_device(): pl.pallas_call(scoped, out_shape=(pltpu.VMEM((width, points), F32), pltpu...  7.72 us
    pallas_call x1, Pallas kernels, on_device(): pl.pallas_call(lambda *refs: pl.run_scoped(functools.partial(finish, n, *...  0.95 us

profile of v8, /device:TPU:0, one launch (start us, length us, event | category | flops | bytes accessed | tf_op | source)
XLA Modules:
  0.0 8.7 jit_solution(6816182464232398291)
XLA Ops:
  0.0 7.7 %shard_map.109 = (f32[55,2197]{1,0:T(8,128)S(1)}, bf16[64,256]{1,0:T(8,128)(2,1)S(1)}, bf16[4,2,256,256]{3,2,1,0:T(8,128)(2,1)S(1)}, bf16[6,64,256]{2,1,0:T(8,128)(2,1)S(1)}) custom-call(s32[1,6]{1,0:T(1,128)} %refs_0_.1, s32[1,6]{1,0:T(1,128)} %refs_1_.1, f32[1,3]{1,0:T(1,128)} %refs_2_.1, f32[55,1,2197]{2,1,0:T(1,128)} %bitcast.2, f32[3,55,55]{2,1,0:T(8,128)} %refs_4_.1, ...), custom_call_target="tpu_custom_call" | custom-call | tf_op jit(solution)/shard_map/pallas_call | solution.py:424
  7.7 0.9 %shard_map.110 = f32[55,1,2197]{2,1,0:T(1,128)} custom-call(f32[55,2197]{1,0:T(8,128)S(1)} %get-tuple-element.9.refs_0_, bf16[64,256]{1,0:T(8,128)(2,1)S(1)} %get-tuple-element.10.refs_1_, bf16[4,2,256,256]{3,2,1,0:T(8,128)(2,1)S(1)} %get-tuple-element.11.refs_2_, bf16[6,64,256]{2,1,0:T(8,128)(2,1)S(1)} %get-tuple-element.12.refs_3_), custom_call_target="tpu_custom_call" | custom-call | tf_op jit(solution)/shard_map/pallas_call | solution.py:454

commit v9 on v8

--- a/solution.py
+++ b/solution.py
@@ -382,19 +382,20 @@
 
 
 def finish(n, part_ref, far_ref, oper, lift_lhs, out_ref, low_ref, sem):
-    width, points = part_ref.shape
+    width = part_ref.shape[0]
     low = low_ref.shape[1]
-    write = lambda a, i, start, stop: pltpu.make_async_copy(
-        a, out_ref.at[:, 0, start:stop], sem.at[i]
-    )
-    inner = write(part_ref.at[:, low:], 0, low, points)
-    inner.start()
+    writes = [pltpu.make_async_copy(part_ref.at[:, low:], out_ref.at[:, 0, low:], sem.at[0])]
+    writes[0].start()
     (term,) = far_terms((0,), lambda f: far_ref[...], oper, lift_lhs, n * n)
-    low_ref[...] = part_ref[:, :low] + term[:width, :low]
-    outer = write(low_ref, 1, 0, low)
-    outer.start()
-    inner.wait()
-    outer.wait()
+    for i, r in enumerate(range(0, width, STRIP)):
+        strip = slice(r, min(r + STRIP, width))
+        low_ref[strip] = part_ref[strip, :low] + term[strip, :low]
+        writes.append(
+            pltpu.make_async_copy(low_ref.at[strip], out_ref.at[strip, 0, :low], sem.at[i + 1])
+        )
+        writes[-1].start()
+    for copy in writes:
+        copy.wait()
 
 
 def solution(mesh):
@@ -453,7 +454,8 @@
         low = -(-plane // 128) * 128
         out = pl.pallas_call(
             lambda *refs: pl.run_scoped(
-                functools.partial(finish, n, *refs), pltpu.SemaphoreType.DMA((2,))
+                functools.partial(finish, n, *refs),
+                pltpu.SemaphoreType.DMA((1 + -(-width // STRIP),)),
             ),
             out_shape=jax.ShapeDtypeStruct(rows.shape, F32),
             in_specs=[vmem_spec] * 4,

time: 8.82 us -> 8.81 us (level)
  no operation moved by 1% of the time
where the time goes in v9:
time: 8.81 us; the launch traced here: 8.67 us
  Pallas kernels  8.66 us (98%)
    pallas_call x1, Pallas kernels, on_device(): pl.pallas_call(scoped, out_shape=(pltpu.VMEM((width, points), F32), pltpu...  7.72 us
    pallas_call x1, Pallas kernels, on_device(): pl.pallas_call(lambda *refs: pl.run_scoped(functools.partial(finish, n, *...  0.94 us

profile of v9, /device:TPU:0, one launch (start us, length us, event | category | flops | bytes accessed | tf_op | source)
XLA Modules:
  0.0 8.7 jit_solution(14279275490787539338)
XLA Ops:
  0.0 7.7 %shard_map.109 = (f32[55,2197]{1,0:T(8,128)S(1)}, bf16[64,256]{1,0:T(8,128)(2,1)S(1)}, bf16[4,2,256,256]{3,2,1,0:T(8,128)(2,1)S(1)}, bf16[6,64,256]{2,1,0:T(8,128)(2,1)S(1)}) custom-call(s32[1,6]{1,0:T(1,128)} %refs_0_.1, s32[1,6]{1,0:T(1,128)} %refs_1_.1, f32[1,3]{1,0:T(1,128)} %refs_2_.1, f32[55,1,2197]{2,1,0:T(1,128)} %bitcast.2, f32[3,55,55]{2,1,0:T(8,128)} %refs_4_.1, ...), custom_call_target="tpu_custom_call" | custom-call | tf_op jit(solution)/shard_map/pallas_call | solution.py:425
  7.7 0.9 %shard_map.110 = f32[55,1,2197]{2,1,0:T(1,128)} custom-call(f32[55,2197]{1,0:T(8,128)S(1)} %get-tuple-element.9.refs_0_, bf16[64,256]{1,0:T(8,128)(2,1)S(1)} %get-tuple-element.10.refs_1_, bf16[4,2,256,256]{3,2,1,0:T(8,128)(2,1)S(1)} %get-tuple-element.11.refs_2_, bf16[6,64,256]{2,1,0:T(8,128)(2,1)S(1)} %get-tuple-element.12.refs_3_), custom_call_target="tpu_custom_call" | custom-call | tf_op jit(solution)/shard_map/pallas_call | solution.py:455

commit v10 on v9

--- a/solution.py
+++ b/solution.py
@@ -281,10 +281,10 @@
         pl.semaphore_signal(ack.at[face ^ 1], inc=1, device_id=across[face], device_id_type=MESH)
     when(jnp.logical_not(before), traces)
     copies[3].start()
+    when(rest, flux_matrices)
+    when(odd & rest, copies[1].start)
     when(rest & y_first, lambda: answer(2))
     when(rest & jnp.logical_not(y_first), lambda: answer(0))
-    when(rest, flux_matrices)
-    when(odd & rest, copies[1].start)
     when(rest, volume_flux)
     when(inner & odd, lambda: answer(0))
     when(inner & even, lambda: answer(2))

time: 8.81 us -> 8.81 us (level)
  no operation moved by 1% of the time
where the time goes in v10:
time: 8.81 us; the launch traced here: 8.67 us
  Pallas kernels  8.66 us (98%)
    pallas_call x1, Pallas kernels, on_device(): pl.pallas_call(scoped, out_shape=(pltpu.VMEM((width, points), F32), pltpu...  7.72 us
    pallas_call x1, Pallas kernels, on_device(): pl.pallas_call(lambda *refs: pl.run_scoped(functools.partial(finish, n, *...  0.94 us

profile of v10, /device:TPU:0, one launch (start us, length us, event | category | flops | bytes accessed | tf_op | source)
XLA Modules:
  0.0 8.7 jit_solution(11814863745653089169)
XLA Ops:
  0.0 7.7 %shard_map.109 = (f32[55,2197]{1,0:T(8,128)S(1)}, bf16[64,256]{1,0:T(8,128)(2,1)S(1)}, bf16[4,2,256,256]{3,2,1,0:T(8,128)(2,1)S(1)}, bf16[6,64,256]{2,1,0:T(8,128)(2,1)S(1)}) custom-call(s32[1,6]{1,0:T(1,128)} %refs_0_.1, s32[1,6]{1,0:T(1,128)} %refs_1_.1, f32[1,3]{1,0:T(1,128)} %refs_2_.1, f32[55,1,2197]{2,1,0:T(1,128)} %bitcast.2, f32[3,55,55]{2,1,0:T(8,128)} %refs_4_.1, ...), custom_call_target="tpu_custom_call" | custom-call | tf_op jit(solution)/shard_map/pallas_call | solution.py:425
  7.7 0.9 %shard_map.110 = f32[55,1,2197]{2,1,0:T(1,128)} custom-call(f32[55,2197]{1,0:T(8,128)S(1)} %get-tuple-element.9.refs_0_, bf16[64,256]{1,0:T(8,128)(2,1)S(1)} %get-tuple-element.10.refs_1_, bf16[4,2,256,256]{3,2,1,0:T(8,128)(2,1)S(1)} %get-tuple-element.11.refs_2_, bf16[6,64,256]{2,1,0:T(8,128)(2,1)S(1)} %get-tuple-element.12.refs_3_), custom_call_target="tpu_custom_call" | custom-call | tf_op jit(solution)/shard_map/pallas_call | solution.py:455
